TPU v7x, 256 devices: a whole 4x4x8 slice. The times are simulated.
256 devices in a mesh: dp: 16 (over x, z_lo), space: 8 (over y, core), chan: 2 (over z_hi).
Axes of the slice: x: 4, y: 4, z: 8 (z_hi: 2, z_lo: 4; z = z_hi * 4 + z_lo), core: 2. Of those that a mesh axis runs over, the one named last changes fastest.
Arguments:
- pixels: bfloat16 [16, 64, 64, 512], P('dp', 'space'), may hold values from -6 to 6
- hidden: bfloat16 [16, 128, 4096], P('dp', None, 'space'), may hold values from -6 to 6
- enc_gain: bfloat16 [4096], replicated, may hold values from 0.099609375 to 1.8984375
- lengths: int32 [16], P('dp'), may hold values from 1 to 128
- time_steps: int32 [16], P('dp'), may hold values from 0 to 999
- attn_gain: bfloat16 [512], replicated, may hold values from 0.099609375 to 1.8984375
- w_query: bfloat16 [512, 512], P(None, 'chan'), may hold values from -1 to 1
- w_key: bfloat16 [4096, 512], P(None, 'chan'), may hold values from -1 to 1
- w_value: bfloat16 [4096, 512], P(None, 'chan'), may hold values from -0.09375 to 0.09375
- w_out: bfloat16 [512, 512], P('chan'), may hold values from -0.25 to 0.25
- w_time: bfloat16 [512, 1024], replicated, may hold values from -0.25 to 0.25
- w_conv: bfloat16 [4608, 512], P(None, 'chan'), may hold values from -0.09375 to 0.09375
- cotangent: bfloat16 [16, 64, 64, 512], P('dp', 'space', None, 'chan'), may hold values from -6 to 6
Outputs:
- result: bfloat16 [16, 64, 64, 512], P('dp', 'space', None, 'chan')
- grad_conv: float32 [4608, 512], P(('dp', 'space'), 'chan')
- grad_out_t: float32 [512, 512], P(('dp', 'space'), 'chan')
All inputs are finite; a program needn't handle non-finite values.
Results may differ from a plain program's by a relative error of at most 0.01.
The roundings to bfloat16 on the way count: a program that leaves them out, or rounds other values in their place, can miss the bound.
Values may be sent and summed in bfloat16 or wider, within the bound.
A program may use at most 128 MiB of HBM per device.

v0:
```python
import math

import jax
import jax.numpy as jnp
from jax import lax
from jax.sharding import Mesh
from jax.sharding import PartitionSpec as P

HEAD_DIM = 64
TEMB = 512
SPACE = ("space_0", "space_1")
DP_SPACE = ("dp_0", "dp_1", "space_0", "space_1")
DP = ("dp_0", "dp_1")


def joined_along(tiles, dim):
    shape = list(tiles.shape[1:])
    shape[dim] *= tiles.shape[0]
    return jnp.moveaxis(tiles, 0, dim).reshape(shape)


def sent_to_all(x, axis):
    copies = jnp.broadcast_to(x, (lax.axis_size(axis), *x.shape))
    return lax.all_to_all(copies, axis, split_axis=0, concat_axis=0, tiled=True)


def gathered_copies(x, axis, dim):
    return joined_along(sent_to_all(x, axis), dim)


def taken_together(x, axis):
    return sent_to_all(x, axis).astype(jnp.float32).sum(axis=0)


def padded_2(cells, sides, width):
    for axis, dim in sides:
        count = lax.axis_size(axis)
        ends = count - 1
        head = lax.slice_in_dim(cells, 0, width, axis=dim)
        tail = lax.slice_in_dim(cells, cells.shape[dim] - width, cells.shape[dim], axis=dim)
        cells = jnp.concatenate(
            [
                lax.ppermute(tail, axis, [(i, (i + 1) % count) for i in range(ends)]),
                cells,
                lax.ppermute(head, axis, [((i + 1) % count, i) for i in range(ends)]),
            ],
            axis=dim,
        )
    return cells


def cut_along(x, dim, devices):
    before, after = (x.shape[:dim], x.shape[dim + 1 :])
    return jnp.moveaxis(x.reshape(*before, devices, -1, *after), dim, 0)


def sum_at_owner(x, axis, dim):
    tiles = cut_along(x, dim, lax.axis_size(axis))
    arrived = lax.all_to_all(tiles, axis, split_axis=0, concat_axis=0, tiled=True)
    return arrived.astype(jnp.float32).sum(axis=0)


def sum_in_two_steps(x, axes, dim):
    far, near = axes
    tiles = cut_along(x, dim, lax.axis_size(far))
    nearer = sum_at_owner(tiles, near, dim + 1)
    arrived = lax.all_to_all(
        nearer.astype(jnp.bfloat16), far, split_axis=0, concat_axis=0, tiled=True
    )
    return arrived.astype(jnp.float32).sum(axis=0)


def rms_scale(source, gain_row):
    source_f = source.astype(jnp.float32)
    mean_sq = jnp.mean(source_f * source_f, axis=-1, keepdims=True)
    return source_f * lax.rsqrt(mean_sq + 1e-06) * gain_row.astype(jnp.float32)


def time_embed(time_steps, emb_width):
    half_width = emb_width // 2
    frequency = jnp.exp(
        -math.log(10000.0) * jnp.arange(half_width).astype(jnp.float32) / half_width
    )
    angles = time_steps.astype(jnp.float32)[:, None] * frequency[None, :]
    return jnp.concatenate([jnp.sin(angles), jnp.cos(angles)], axis=1).astype(jnp.bfloat16)


def tap_stack(padded, row_count, col_count, flipped):
    tap_parts = []
    for tap_row in range(3):
        for tap_col in range(3):
            start_row = 2 - tap_row if flipped else tap_row
            start_col = 2 - tap_col if flipped else tap_col
            tap_parts.append(
                padded[:, start_row : start_row + row_count, start_col : start_col + col_count, :]
            )
    return jnp.concatenate(tap_parts, axis=-1)


def shards(
    pixels,
    hidden,
    enc_gain,
    lengths,
    time_steps,
    attn_gain,
    w_query,
    w_key,
    w_value,
    w_out,
    w_time,
    w_conv,
    cotangent,
):
    img_dev, row_count, col_count, full_width = pixels.shape
    local_width = w_query.shape[1]
    heads_here = local_width // HEAD_DIM
    cap_len = hidden.shape[1]
    pixel_count = row_count * col_count
    gathered = gathered_copies(hidden, SPACE, 2)
    context = rms_scale(gathered, enc_gain).astype(jnp.bfloat16)
    key_proj = jnp.einsum("cle,ef->clf", context, w_key, preferred_element_type=jnp.float32).astype(
        jnp.bfloat16
    )
    value_proj = jnp.einsum(
        "cle,ef->clf", context, w_value, preferred_element_type=jnp.float32
    ).astype(jnp.bfloat16)
    flat_pix = pixels.reshape(img_dev, pixel_count, full_width)
    normed = rms_scale(flat_pix, attn_gain).astype(jnp.bfloat16)
    query_proj = jnp.einsum(
        "bpc,cf->bpf", normed, w_query, preferred_element_type=jnp.float32
    ).astype(jnp.bfloat16)
    query_heads = query_proj.reshape(img_dev, pixel_count, heads_here, HEAD_DIM)
    key_heads = key_proj.reshape(img_dev, cap_len, heads_here, HEAD_DIM)
    value_heads = value_proj.reshape(img_dev, cap_len, heads_here, HEAD_DIM)
    scores = jnp.einsum(
        "bphd,bjhd->bhpj", query_heads, key_heads, preferred_element_type=jnp.float32
    ) * HEAD_DIM ** (-0.5)
    key_live = jnp.arange(cap_len)[None, :] < lengths[:, None]
    scores = jnp.where(key_live[:, None, None, :], scores, -1e30)
    weights_soft = jax.nn.softmax(scores, axis=-1).astype(jnp.bfloat16)
    attended = jnp.einsum(
        "bhpj,bjhd->bphd", weights_soft, value_heads, preferred_element_type=jnp.float32
    )
    attended = attended.astype(jnp.bfloat16).reshape(img_dev, pixel_count, local_width)
    head_part = jnp.einsum("bpf,fc->bpc", attended, w_out, preferred_element_type=jnp.float32)
    head_sum = taken_together(head_part.astype(jnp.bfloat16), "chan").astype(jnp.float32)
    mixed_res = flat_pix.astype(jnp.float32) + head_sum
    film_out = jnp.dot(time_embed(time_steps, TEMB), w_time, preferred_element_type=jnp.float32)
    film_scale = film_out[:, None, :full_width]
    film_shift = film_out[:, None, full_width:]
    lifted = mixed_res * (1.0 + film_scale) + film_shift
    activation = (
        jax.nn.silu(lifted).astype(jnp.bfloat16).reshape(img_dev, row_count, col_count, full_width)
    )
    rimmed = padded_2(activation, ((SPACE, 1),), 1)
    padded = jnp.pad(rimmed, ((0, 0), (0, 0), (1, 1), (0, 0)))
    patches = tap_stack(padded, row_count, col_count, False).reshape(-1, 9 * full_width)
    conv_out = jnp.dot(patches, w_conv, preferred_element_type=jnp.float32)
    chan_start = lax.axis_index("chan") * local_width
    own_part = lax.dynamic_slice_in_dim(
        mixed_res.reshape(-1, full_width), chan_start, local_width, 1
    )
    result = (
        (own_part + conv_out)
        .astype(jnp.bfloat16)
        .reshape(img_dev, row_count, col_count, local_width)
    )
    cot_rimmed = padded_2(cotangent, ((SPACE, 1),), 1)
    cot_padded = jnp.pad(cot_rimmed, ((0, 0), (0, 0), (1, 1), (0, 0)))
    cot_patches = tap_stack(cot_padded, row_count, col_count, True).reshape(-1, 9 * local_width)
    w_back = (
        w_conv.reshape(9, full_width, local_width)
        .transpose(0, 2, 1)
        .reshape(9 * local_width, full_width)
    )
    grad_act = taken_together(
        jnp.dot(cot_patches, w_back, preferred_element_type=jnp.float32).astype(jnp.bfloat16),
        "chan",
    ).astype(jnp.float32)
    cot_full = gathered_copies(cotangent, "chan", 3).reshape(img_dev, pixel_count, full_width)
    grad_act = grad_act.reshape(img_dev, pixel_count, full_width)
    sigmoid_u = jax.nn.sigmoid(lifted)
    grad_lift = grad_act * sigmoid_u * (1.0 + lifted * (1.0 - sigmoid_u))
    grad_mixed = (cot_full.astype(jnp.float32) + grad_lift * (1.0 + film_scale)).astype(
        jnp.bfloat16
    )
    cot_flat = cotangent.reshape(-1, local_width)
    conv_term = lax.dot_general(
        patches, cot_flat, (((0,), (0,)), ((), ())), preferred_element_type=jnp.float32
    )
    out_term = lax.dot_general(
        grad_mixed.reshape(-1, full_width),
        attended.reshape(-1, local_width),
        (((0,), (0,)), ((), ())),
        preferred_element_type=jnp.float32,
    )
    grad_conv, grad_out_t = (
        sum_in_two_steps(
            conv_term.astype(jnp.bfloat16), (("dp_0", "dp_1", "space_0"), "space_1"), 0
        ),
        sum_in_two_steps(
            out_term.astype(jnp.bfloat16), (("dp_0", "dp_1", "space_0"), "space_1"), 0
        ),
    )
    return (result, grad_conv, grad_out_t)


def solution(mesh):
    finer = Mesh(
        mesh.devices.reshape(4, 4, 4, 2, mesh.shape["chan"]),
        ("dp_0", "dp_1", "space_0", "space_1", "chan"),
    )
    placed = (
        P(DP, SPACE, None, None),
        P(DP, None, SPACE),
        P(),
        P(DP),
        P(DP),
        P(),
        P(None, "chan"),
        P(None, "chan"),
        P(None, "chan"),
        P("chan", None),
        P(),
        P(None, "chan"),
        P(DP, SPACE, None, "chan"),
    )
    return jax.shard_map(
        shards,
        mesh=finer,
        in_specs=placed,
        out_specs=(P(DP, SPACE, None, "chan"), P(DP_SPACE, "chan"), P(DP_SPACE, "chan")),
        check_vma=False,
    )
```

profile of v0, /device:TPU:1, one launch (start us, length us, event | category | flops | bytes accessed | tf_op | source)
XLA Modules:
  0.0 206.4 jit_solution(7733396519817346189)
XLA Ops:
  0.7 1.2 copy.99
  1.8 1.1 broadcast_in_dim.20
  3.0 6.7 %all-to-all-start = ((bf16[8,1,128,512]{2,3,1,0:T(8,128)(2,1)}), bf16[8,1,128,512]{2,3,1,0:T(8,128)(2,1)S(1)}, u32[]{:S(2)}, u32[]{:S(2)}) async-start(bf16[8,1,128,512]{2,3,1,0:T(8,128)(2,1)} %broadcast_in_dim.20), calls=%async_computation | async-start | bytes 2097152 | tf_op jit(solution)/shard_map/all_to_all | solution.py:24
  9.6 3.5 %collective-permute-start.2 = (bf16[1,1,64,256]{3,2,1,0:T(8,128)(2,1)S(1)}, bf16[1,1,64,256]{3,2,1,0:T(8,128)(2,1)S(1)}, u32[]{:S(2)}, u32[]{:S(2)}) collective-permute-start(bf16[1,1,64,256]{3,2,1,0:T(8,128)(2,1)S(1)} %get-tuple-element.7), channel_id=1, source_target_pairs={{0,2},{2,4},{4,6},{6,8},{8,10},{10,12},{12,14},{1,3},{3,5},{5,7},{... | collective-permute-start | bytes 98312 | tf_op jit(solution)/shard_map/ppermute | solution.py:43
  13.2 1.9 collective-permute-start.3
  15.1 1.2 multiply_reduce_fusion.1
  17.1 1.2 fusion.14
  18.3 2.0 convolution_convert_fusion.4
  21.5 4.3 %copy.106 = bf16[9,256,512]{2,1,0:T(8,128)(2,1)} copy(bf16[9,256,512]{1,2,0:T(8,128)(2,1)} %bitcast.105) | data formatting | bytes 4718592 | tf_op jit(solution)/shard_map/transpose | solution.py:174
  26.3 1.3 copy-done.5
  27.6 2.2 %convolution_convert_fusion.1 = bf16[512,512]{1,0:T(8,128)(2,1)} fusion(bf16[512,2304]{1,0:T(8,128)(2,1)S(1)} %bitcast.119, bf16[2304,512]{1,0:T(8,128)(2,1)S(1)} %bitcast.106), kind=kOutput, calls=%fused_computation.19 | convolution fusion | flops 1208221696 | bytes 5242880 | tf_op jit(solution)/shard_map/dot_general | solution.py:178
  29.8 2.1 %broadcast_in_dim.42 = bf16[2,512,512]{2,1,0:T(8,128)(2,1)} broadcast(bf16[512,512]{1,0:T(8,128)(2,1)} %convolution_convert_fusion.1), dimensions={1,2} | broadcast | bytes 1572864 | tf_op jit(solution)/shard_map/broadcast_in_dim | solution.py:23
  31.9 7.5 %all-to-all-start.5 = ((bf16[2,512,512]{2,1,0:T(8,128)(2,1)}), bf16[2,512,512]{2,1,0:T(8,128)(2,1)}, u32[]{:S(2)}, u32[]{:S(2)}) async-start(bf16[2,512,512]{2,1,0:T(8,128)(2,1)} %broadcast_in_dim.42), calls=%async_computation.5 | async-start | bytes 2097152 | tf_op jit(solution)/shard_map/all_to_all | solution.py:24
  41.6 1.0 copy-done.6
  44.1 1.3 fusion.8
  45.4 1.1 convolution_convert_fusion.3
  46.5 1.4 convolution_convert_fusion
  47.9 18.7 %all-to-all-done.5 = bf16[2,512,512]{2,1,0:T(8,128)(2,1)} async-done(((bf16[2,512,512]{2,1,0:T(8,128)(2,1)}), bf16[2,512,512]{2,1,0:T(8,128)(2,1)}, u32[]{:S(2)}, u32[]{:S(2)}) %all-to-all-start.5) | async-done | bytes 1048608 | tf_op jit(solution)/shard_map/all_to_all | solution.py:24
  66.6 1.1 broadcast_in_dim.23
  67.7 4.4 %all-to-all-start.1 = ((bf16[2,1,512,512]{3,2,1,0:T(8,128)(2,1)}), bf16[2,1,512,512]{3,2,1,0:T(8,128)(2,1)}, u32[]{:S(2)}, u32[]{:S(2)}) async-start(bf16[2,1,512,512]{3,2,1,0:T(8,128)(2,1)} %broadcast_in_dim.23), calls=%async_computation.1 | async-start | bytes 2097152 | tf_op jit(solution)/shard_map/all_to_all | solution.py:24
  72.1 1.1 convert_element_type.217
  74.0 1.5 fusion.41
  75.5 1.5 convert_reduce_fusion.1
  77.0 1.6 reduce_sum.104
  78.6 10.5 %all-to-all-done.1 = bf16[2,1,512,512]{3,2,1,0:T(8,128)(2,1)} async-done(((bf16[2,1,512,512]{3,2,1,0:T(8,128)(2,1)}), bf16[2,1,512,512]{3,2,1,0:T(8,128)(2,1)}, u32[]{:S(2)}, u32[]{:S(2)}) %all-to-all-start.1) | async-done | bytes 1048608 | tf_op jit(solution)/shard_map/all_to_all | solution.py:24
  90.1 4.2 %all-to-all-start.4 = ((bf16[2,1,8,64,256]{4,3,2,1,0:T(8,128)(2,1)}), bf16[2,1,8,64,256]{4,3,2,1,0:T(8,128)(2,1)}, u32[]{:S(2)}, u32[]{:S(2)}) async-start(bf16[2,1,8,64,256]{4,3,2,1,0:T(8,128)(2,1)} %broadcast_in_dim.24), calls=%async_computation.4 | async-start | bytes 1048576 | tf_op jit(solution)/shard_map/all_to_all | solution.py:24
  94.3 1.5 convert_reduce_fusion.2
  95.8 1.7 reduce_sum.105
  97.5 1.7 multiply_convert_fusion
  99.9 6.6 %collective-permute-start = (bf16[1,1,64,512]{3,2,1,0:T(8,128)(2,1)}, bf16[1,1,64,512]{3,2,1,0:T(8,128)(2,1)S(1)}, u32[]{:S(2)}, u32[]{:S(2)}) collective-permute-start(bf16[1,1,64,512]{3,2,1,0:T(8,128)(2,1)} %get-tuple-element.5), channel_id=1, source_target_pairs={{0,2},{2,4},{4,6},{6,8},{8,10},{10,12},{12,14},{1,3},{3,5},{5,7},{... | collective-permute-start | bytes 196616 | tf_op jit(solution)/shard_map/ppermute | solution.py:43
  106.4 1.9 collective-permute-start.1
  108.4 2.6 %fusion.12 = bf16[1,8,64,2,256]{4,2,1,0,3:T(8,128)(2,1)S(1)} fusion(f32[1,8,64,2,256]{4,3,2,1,0:T(2,128)} %reduce_sum.104, bf16[2,1,8,64,256]{4,3,2,1,0:T(8,128)(2,1)} %all-to-all-done.4, f32[1,8,64,2,256]{4,3,2,1,0:T(2,128)} %reduce_sum.105, f32[1,8,8,2,8,256]{5,4,3,2,1,0:T(8,128)} %bitcast.103, f32[2,256]{1,0:T(2,128)S(1)} %add.155, f32[2,256]{1,0:T(2,128)S(1)} %add.154), kind=kLoop, calls=%fused_computation.33 | loop fusion | flops 3932160 | bytes 4198400 | tf_op jit(solution)/shard_map/convert_element_type | solution.py:185
  111.6 1.1 convolution_convert_fusion.2
  112.7 1.0 reshape_reshape.9
  113.8 3.8 %all_to_all.40 = bf16[2,64,4,256]{3,2,1,0:T(4,128)(2,1)S(1)} all-to-all(bf16[2,64,4,256]{3,2,1,0:T(4,128)(2,1)S(1)} %bitcast.111), channel_id=1, replica_groups=mesh['dp_0'=4,'dp_1'=4,'space_0'=4,'space_1'=2,'chan'=2] {'space_1'}, dimensions={0} | all-to-all | bytes 524288 | tf_op jit(solution)/shard_map/all_to_all | solution.py:59
  119.3 2.1 %copy-done.9 = bf16[1,8,64,4608]{3,2,1,0:T(8,128)(2,1)} copy-done((bf16[1,8,64,4608]{3,2,1,0:T(8,128)(2,1)}, bf16[1,8,64,4608]{3,2,1,0:T(8,128)(2,1)S(1)}, u32[]{:S(2)}) %copy-start.9) | copy-done | bytes 4718616
  121.4 2.9 %fusion.1 = bf16[4608,256]{1,0:T(8,128)(2,1)} fusion(bf16[1,8,64,4608]{3,2,1,0:T(8,128)(2,1)S(1)} %slice_dynamic-update-slice_fusion, bf16[1,8,64,256]{3,2,1,0:T(8,128)(2,1)S(1)} %copy-done.4), kind=kOutput, calls=%fused_computation.2 | convolution fusion | flops 1209139200 | bytes 7340032 | tf_op jit(solution)/shard_map/dot_general | solution.py:189
  124.4 4.7 %reshape_reshape.8 = bf16[64,2,36,256]{3,2,1,0:T(8,128)(2,1)} reshape(bf16[4608,256]{1,0:T(8,128)(2,1)} %fusion.1) | data formatting | bytes 4718592 | tf_op jit(solution)/shard_map/reshape;reshape | solution.py:54
  129.1 2.6 %copy.104 = bf16[2,64,36,256]{3,1,2,0:T(8,128)(2,1)S(1)} copy(bf16[2,64,36,256]{3,2,0,1:T(8,128)(2,1)} %bitcast.99) | data formatting | bytes 4718592 | tf_op jit(solution)/shard_map/transpose | solution.py:54
  131.6 6.6 %all_to_all.41 = bf16[2,64,36,256]{3,1,2,0:T(8,128)(2,1)} all-to-all(bf16[2,64,36,256]{3,1,2,0:T(8,128)(2,1)S(1)} %copy.104), channel_id=1, replica_groups=mesh['dp_0'=4,'dp_1'=4,'space_0'=4,'space_1'=2,'chan'=2] {'space_1'}, dimensions={0} | all-to-all | bytes 4718592 | tf_op jit(solution)/shard_map/all_to_all | solution.py:59
  138.2 15.7 %all-to-all-start.7 = ((bf16[64,4,256]{2,1,0:T(4,128)(2,1)}), bf16[64,4,256]{2,1,0:T(4,128)(2,1)S(1)}, u32[]{:S(2)}, u32[]{:S(2)}) async-start(bf16[64,4,256]{2,1,0:T(4,128)(2,1)} %reduce_sum.106), calls=%async_computation.7 | async-start | bytes 262144 | tf_op jit(solution)/shard_map/all_to_all | solution.py:67
  153.9 3.5 %reduce_sum.101 = bf16[64,36,256]{2,0,1:T(8,128)(2,1)} reduce(bf16[2,64,36,256]{3,1,2,0:T(8,128)(2,1)} %all_to_all.41, bf16[]{:T(256)} %constant.43.clone.1), dimensions={0}, to_apply=%region_5.6 | reduce | flops 589824 | bytes 3538946 | tf_op jit(solution)/shard_map/reduce_sum | solution.py:60
  157.4 3.1 %copy.105 = bf16[64,36,256]{2,1,0:T(8,128)(2,1)} copy(bf16[64,36,256]{2,0,1:T(8,128)(2,1)} %reduce_sum.101) | data formatting | bytes 2359296 | tf_op jit(solution)/shard_map/reduce_sum | solution.py:60
  160.6 2.9 %all-to-all-done.7 = bf16[64,4,256]{2,1,0:T(4,128)(2,1)S(1)} async-done(((bf16[64,4,256]{2,1,0:T(4,128)(2,1)}), bf16[64,4,256]{2,1,0:T(4,128)(2,1)S(1)}, u32[]{:S(2)}, u32[]{:S(2)}) %all-to-all-start.7) | async-done | bytes 131104 | tf_op jit(solution)/shard_map/all_to_all | solution.py:67
  163.4 7.5 %all-to-all-start.3 = ((bf16[64,36,256]{2,1,0:T(8,128)(2,1)}), bf16[64,36,256]{2,1,0:T(8,128)(2,1)}, u32[]{:S(2)}, u32[]{:S(2)}) async-start(bf16[64,36,256]{2,1,0:T(8,128)(2,1)} %copy.105), calls=%async_computation.3 | async-start | bytes 2621440 | tf_op jit(solution)/shard_map/all_to_all | solution.py:67
  170.9 5.2 %fusion.9 = bf16[512,256]{1,0:T(8,128)(2,1)} fusion(bf16[512,4608]{1,0:T(8,128)(2,1)} %bitcast.118, bf16[4608,256]{1,0:T(8,128)(2,1)} %param.24, f32[1,512,512]{2,1,0:T(8,128)S(1)} %bitcast.101, s32[]{:T(128)S(6)} %select_n.9, f32[1,512,512]{2,1,0:T(8,128)} %bitcast.104), kind=kOutput, calls=%fused_computation.21 | convolution fusion | flops 1208352768 | bytes 8388612 | tf_op jit(solution)/shard_map/dot_general | solution.py:159
  176.7 27.5 %all-to-all-done.3 = bf16[64,36,256]{2,1,0:T(8,128)(2,1)} async-done(((bf16[64,36,256]{2,1,0:T(8,128)(2,1)}), bf16[64,36,256]{2,1,0:T(8,128)(2,1)}, u32[]{:S(2)}, u32[]{:S(2)}) %all-to-all-start.3) | async-done | bytes 1179680 | tf_op jit(solution)/shard_map/all_to_all | solution.py:67
  204.2 2.2 %convert_reduce_fusion = f32[36,256]{1,0:T(8,128)} fusion(bf16[64,36,256]{2,1,0:T(8,128)(2,1)} %all-to-all-done.3), kind=kLoop, calls=%fused_computation.4 | loop fusion | flops 1170432 | bytes 1216512 | tf_op jit(solution)/shard_map/reduce_sum | solution.py:70
  (75 shorter events, 10.0 us)
Async XLA Ops:
  0.6 40.3 %copy-start = (bf16[4096,256]{1,0:T(8,128)(2,1)S(1)}, bf16[4096,256]{1,0:T(8,128)(2,1)}, u32[]{:S(2)}) copy-start(bf16[4096,256]{1,0:T(8,128)(2,1)} %param.20) | copy-start | bytes 6291460
  0.6 9.0 %copy-start.4 = (bf16[1,8,64,256]{3,2,1,0:T(8,128)(2,1)S(1)}, bf16[1,8,64,256]{3,2,1,0:T(8,128)(2,1)}, u32[]{:S(2)}) copy-start(bf16[1,8,64,256]{3,2,1,0:T(8,128)(2,1)} %param.25) | copy-start | bytes 786436
  0.7 15.8 %copy-start.10 = (bf16[512]{0:T(512)(128)(2,1)S(1)}, bf16[512]{0:T(512)(128)(2,1)}, u32[]{:S(2)}) copy-start(bf16[512]{0:T(512)(128)(2,1)} %param.18) | copy-start | bytes 3076
  3.0 26.8 %all-to-all-start = ((bf16[8,1,128,512]{2,3,1,0:T(8,128)(2,1)}), bf16[8,1,128,512]{2,3,1,0:T(8,128)(2,1)S(1)}, u32[]{:S(2)}, u32[]{:S(2)}) async-start(bf16[8,1,128,512]{2,3,1,0:T(8,128)(2,1)} %broadcast_in_dim.20), calls=%async_computation | async-start | bytes 2097152 | tf_op jit(solution)/shard_map/all_to_all | solution.py:24
  9.6 16.2 %collective-permute-start.2 = (bf16[1,1,64,256]{3,2,1,0:T(8,128)(2,1)S(1)}, bf16[1,1,64,256]{3,2,1,0:T(8,128)(2,1)S(1)}, u32[]{:S(2)}, u32[]{:S(2)}) collective-permute-start(bf16[1,1,64,256]{3,2,1,0:T(8,128)(2,1)S(1)} %get-tuple-element.7), channel_id=1, source_target_pairs={{0,2},{2,4},{4,6},{6,8},{8,10},{10,12},{12,14},{1,3},{3,5},{5,7},{... | collective-permute-start | bytes 98312 | tf_op jit(solution)/shard_map/ppermute | solution.py:43
  13.2 12.6 %collective-permute-start.3 = (bf16[1,1,64,256]{3,2,1,0:T(8,128)(2,1)S(1)}, bf16[1,1,64,256]{3,2,1,0:T(8,128)(2,1)S(1)}, u32[]{:S(2)}, u32[]{:S(2)}) collective-permute-start(bf16[1,1,64,256]{3,2,1,0:T(8,128)(2,1)S(1)} %get-tuple-element.8), channel_id=1, source_target_pairs={{2,0},{4,2},{6,4},{8,6},{10,8},{12,10},{14,12},{3,1},{5,3},{7,5},{... | collective-permute-start | bytes 98312 | tf_op jit(solution)/shard_map/ppermute | solution.py:45
  25.9 1.7 copy-start.5
  31.9 34.7 %all-to-all-start.5 = ((bf16[2,512,512]{2,1,0:T(8,128)(2,1)}), bf16[2,512,512]{2,1,0:T(8,128)(2,1)}, u32[]{:S(2)}, u32[]{:S(2)}) async-start(bf16[2,512,512]{2,1,0:T(8,128)(2,1)} %broadcast_in_dim.42), calls=%async_computation.5 | async-start | bytes 2097152 | tf_op jit(solution)/shard_map/all_to_all | solution.py:24
  41.0 1.6 copy-start.6
  42.6 0.9 copy-start.7
  42.6 1.0 copy-start.11
  46.5 25.7 %copy-start.3 = (bf16[1,8,64,512]{3,2,1,0:T(8,128)(2,1)S(1)}, bf16[1,8,64,512]{3,2,1,0:T(8,128)(2,1)}, u32[]{:S(2)}) copy-start(bf16[1,8,64,512]{3,2,1,0:T(8,128)(2,1)} %param.13) | copy-start | bytes 1572868
  67.7 21.5 %all-to-all-start.1 = ((bf16[2,1,512,512]{3,2,1,0:T(8,128)(2,1)}), bf16[2,1,512,512]{3,2,1,0:T(8,128)(2,1)}, u32[]{:S(2)}, u32[]{:S(2)}) async-start(bf16[2,1,512,512]{3,2,1,0:T(8,128)(2,1)} %broadcast_in_dim.23), calls=%async_computation.1 | async-start | bytes 2097152 | tf_op jit(solution)/shard_map/all_to_all | solution.py:24
  90.1 18.3 %all-to-all-start.4 = ((bf16[2,1,8,64,256]{4,3,2,1,0:T(8,128)(2,1)}), bf16[2,1,8,64,256]{4,3,2,1,0:T(8,128)(2,1)}, u32[]{:S(2)}, u32[]{:S(2)}) async-start(bf16[2,1,8,64,256]{4,3,2,1,0:T(8,128)(2,1)} %broadcast_in_dim.24), calls=%async_computation.4 | async-start | bytes 1048576 | tf_op jit(solution)/shard_map/all_to_all | solution.py:24
  95.8 1.7 copy-start.1
  99.9 18.6 %collective-permute-start = (bf16[1,1,64,512]{3,2,1,0:T(8,128)(2,1)}, bf16[1,1,64,512]{3,2,1,0:T(8,128)(2,1)S(1)}, u32[]{:S(2)}, u32[]{:S(2)}) collective-permute-start(bf16[1,1,64,512]{3,2,1,0:T(8,128)(2,1)} %get-tuple-element.5), channel_id=1, source_target_pairs={{0,2},{2,4},{4,6},{6,8},{8,10},{10,12},{12,14},{1,3},{3,5},{5,7},{... | collective-permute-start | bytes 196616 | tf_op jit(solution)/shard_map/ppermute | solution.py:43
  106.4 12.0 %collective-permute-start.1 = (bf16[1,1,64,512]{3,2,1,0:T(8,128)(2,1)}, bf16[1,1,64,512]{3,2,1,0:T(8,128)(2,1)S(1)}, u32[]{:S(2)}, u32[]{:S(2)}) collective-permute-start(bf16[1,1,64,512]{3,2,1,0:T(8,128)(2,1)} %get-tuple-element.6), channel_id=1, source_target_pairs={{2,0},{4,2},{6,4},{8,6},{10,8},{12,10},{14,12},{3,1},{5,3},{7,5},{... | collective-permute-start | bytes 196616 | tf_op jit(solution)/shard_map/ppermute | solution.py:45
  108.4 3.3 %copy-start.8 = (bf16[4,64,512]{2,1,0:T(8,128)(2,1)S(1)}, bf16[4,64,512]{2,1,0:T(8,128)(2,1)}, u32[]{:S(2)}) copy-start(bf16[4,64,512]{2,1,0:T(8,128)(2,1)} %convolution_convert_fusion.3) | copy-start | bytes 786436
  119.3 2.1 %copy-start.9 = (bf16[1,8,64,4608]{3,2,1,0:T(8,128)(2,1)}, bf16[1,8,64,4608]{3,2,1,0:T(8,128)(2,1)S(1)}, u32[]{:S(2)}) copy-start(bf16[1,8,64,4608]{3,2,1,0:T(8,128)(2,1)S(1)} %slice_dynamic-update-slice_fusion) | copy-start | bytes 14155780
  138.2 25.3 %all-to-all-start.7 = ((bf16[64,4,256]{2,1,0:T(4,128)(2,1)}), bf16[64,4,256]{2,1,0:T(4,128)(2,1)S(1)}, u32[]{:S(2)}, u32[]{:S(2)}) async-start(bf16[64,4,256]{2,1,0:T(4,128)(2,1)} %reduce_sum.106), calls=%async_computation.7 | async-start | bytes 262144 | tf_op jit(solution)/shard_map/all_to_all | solution.py:67
  157.4 13.5 %copy-start.2 = (f32[512,512]{1,0:T(8,128)S(1)}, f32[512,512]{1,0:T(8,128)}, u32[]{:S(2)}) copy-start(f32[512,512]{1,0:T(8,128)} %copy-done.1) | copy-start | bytes 3145732
  163.4 40.8 %all-to-all-start.3 = ((bf16[64,36,256]{2,1,0:T(8,128)(2,1)}), bf16[64,36,256]{2,1,0:T(8,128)(2,1)}, u32[]{:S(2)}, u32[]{:S(2)}) async-start(bf16[64,36,256]{2,1,0:T(8,128)(2,1)} %copy.105), calls=%async_computation.3 | async-start | bytes 2621440 | tf_op jit(solution)/shard_map/all_to_all | solution.py:67
where the time goes:
time: 208 us; the launch traced here: 206 us
  starting transfers between devices  59.9 us (29%)
  waiting for transfers between devices  59.7 us (29%)
  local copies, waits for them, and re-layouts  32.4 us (16%)
  other arithmetic  21.3 us (10%)
  matrix products  20.3 us (10%)
  blocking collectives  10.3 us (5%)
  between operations  2.44 us (1%)
    all_to_all x2, waiting for transfers between devices, sum_in_two_steps(): lax.all_to_all(nearer.astype(jnp.bfloat16), far, split_axis=0, concat_axi...  30.4 us
    all_to_all x4, waiting for transfers between devices, sent_to_all(): return lax.all_to_all(copies, axis, split_axis=0, concat_axis=0, tiled=True)  29.3 us
    all_to_all x2, starting transfers between devices, sum_in_two_steps(): lax.all_to_all(nearer.astype(jnp.bfloat16), far, split_axis=0, concat_axi...  23.2 us
    all_to_all x4, starting transfers between devices, sent_to_all(): return lax.all_to_all(copies, axis, split_axis=0, concat_axis=0, tiled=True)  22.8 us
    all_to_all x2, blocking collectives, sum_at_owner(): lax.all_to_all(tiles, axis, split_axis=0, concat_axis=0, tiled=True)  10.3 us
    ppermute x2, starting transfers between devices, padded_2(): lax.ppermute(tail, axis, [(i, (i + 1) % count) for i in range(ends)])  10.1 us
    another operation x3, local copies, waits for them, and re-layouts, cut_along(): return jnp.moveaxis(x.reshape(*before, devices, -1, *after), dim, 0)  5.81 us
    unnamed x37, local copies, waits for them, and re-layouts  5.3 us
  transfers between devices with their start and end apart: 10, of which 4 were waited for; matrix products, arithmetic and copies ran while one was open for 24% of the time, Pallas kernels for 0%

commit v1 on v0

v1 whole, which is shorter than its diff:
```python
import math

import jax
import jax.numpy as jnp
from jax import lax
from jax.experimental import pallas as pl
from jax.experimental.pallas import tpu as pltpu
from jax.sharding import Mesh
from jax.sharding import PartitionSpec as P

TEMB = 512
SPACE = ("space_0", "space_1")
DP_SPACE = ("dp_0", "dp_1", "space_0", "space_1")
DP = ("dp_0", "dp_1")
F32 = jnp.float32
BF16 = jnp.bfloat16
MESH = pl.DeviceIdType.MESH

ROWS = 8
COLS = 64
PIX = ROWS * COLS
EXT = PIX + 2 * COLS
CH = 512
HALF = 256
TOK = 128
PIECE = 16
STEP = 128


def dot(a, b):
    return jnp.dot(a, b, preferred_element_type=F32)


def dot_nt(a, b):
    return lax.dot_general(a, b, (((1,), (1,)), ((), ())), preferred_element_type=F32)


def dot_tn(a, b):
    return lax.dot_general(a, b, (((0,), (0,)), ((), ())), preferred_element_type=F32)


def silu_gate(lifted):
    return 1.0 / (1.0 + jnp.exp(-lifted))


def shifted_columns(wide, store):
    col = lax.rem(lax.broadcasted_iota(jnp.int32, wide.shape, 0), COLS)
    down = pltpu.roll(wide, 1, 0)
    up = pltpu.roll(wide, wide.shape[0] - 1, 0)
    store(0, jnp.where(col == 0, 0.0, down).astype(BF16))
    store(1, wide.astype(BF16))
    store(2, jnp.where(col == COLS - 1, 0.0, up).astype(BF16))


def block_rows(tap):
    pieces = []
    row = tap * CH
    while row < (tap + 1) * CH:
        block, inside = divmod(row, 72)
        count = min(72 - inside, (tap + 1) * CH - row)
        pieces.append((block, inside, row - tap * CH, count))
        row += count
    return pieces


def place_of(half, block):
    x, z, y = block // 16, (block // 4) % 4, block % 4
    return x * 16 + y * 4 + z if half == 0 else y * 16 + x * 4 + z


def kernel(
    lengths,
    pix_in,
    hid_in,
    small,
    wq_in,
    wk_in,
    wv_in,
    wo_in,
    wt_in,
    wc_in,
    cot_in,
    res_out,
    gconv_out,
    gout_out,
    pix,
    cot,
    hid,
    wq,
    wk,
    wv,
    wo,
    wt,
    wc,
    kv,
    film,
    att,
    mix,
    act3,
    cot3,
    gact_send,
    gact_recv,
    gact_own,
    result,
    cv,
    core_send,
    core_recv,
    s1,
    r1,
    a1,
    s2,
    r2,
    a2,
    s3,
    r3,
    a3,
    conv_peer,
    out_peer,
    load_sem,
    send_sem,
    recv_sem,
):
    x = lax.axis_index("dp_0")
    z = lax.axis_index("dp_1")
    y = lax.axis_index("space_0")
    core = lax.axis_index("space_1")
    chan = lax.axis_index("chan")
    other = 1 - chan
    slab = y * 2 + core
    count = [0]

    def remote(src, dst, device):
        i = count[0]
        count[0] += 1
        return pltpu.make_async_remote_copy(
            src_ref=src,
            dst_ref=dst,
            send_sem=send_sem.at[i],
            recv_sem=recv_sem.at[i],
            device_id=device,
            device_id_type=MESH,
        )

    def slab_device(d):
        s = lax.rem(slab + d, 8)
        return {"space_0": s // 2, "space_1": lax.rem(s, 2)}

    u = x * (1 - core) + y * core
    v = y * (1 - core) + x * core

    def first_device(d):
        t = lax.rem(u + d, 4)
        return {"dp_0": t * (1 - core) + x * core, "space_0": y * (1 - core) + t * core}

    def second_device(d):
        t = lax.rem(v + d, 4)
        return {"dp_0": x * (1 - core) + t * core, "space_0": t * (1 - core) + y * core}

    def depth_device(d):
        return {"dp_1": lax.rem(z + d, 4)}

    peer_chan = {"chan": other}
    peer_core = {"space_1": 1 - core}
    half_x, low_x = x // 2, lax.rem(x, 2)
    dest = [{"dp_0": 2 * chan + low_x, "space_1": k, "chan": 1 - half_x} for k in range(2)]
    source = [{"dp_0": 2 * (1 - chan) + low_x, "space_1": k, "chan": half_x} for k in range(2)]

    barrier = pltpu.get_barrier_semaphore()
    greeted = (
        [slab_device(d) for d in range(1, 8)]
        + [peer_chan]
        + [{"dp_0": lax.rem(x + d, 4)} for d in range(1, 4)]
        + [depth_device(d) for d in range(1, 4)]
        + dest
        + source
    )
    for device in greeted:
        pl.semaphore_signal(barrier, inc=1, device_id=device, device_id_type=MESH)

    loads = []

    def load(src, dst):
        copy = pltpu.make_async_copy(src, dst, load_sem.at[len(loads)])
        copy.start()
        loads.append(copy)
        return copy

    ld_cot = load(cot_in, cot.at[COLS : COLS + PIX, :])
    ld_hid = load(hid_in.at[pl.ds(slab * PIECE, PIECE), :], hid.at[slab])
    ld_wc = load(wc_in, wc)
    ld_pix = load(pix_in, pix.at[COLS : COLS + PIX, :])
    ld_wk = load(wk_in, wk)
    ld_wv = load(wv_in, wv)
    ld_wq = load(wq_in, wq.at[chan])
    ld_wo = load(wo_in, wo.at[chan])
    ld_wt = load(wt_in, wt)

    pl.semaphore_wait(barrier, len(greeted))

    hid_copies = []
    for d in range(1, 8):
        s = lax.rem(slab + d, 8)
        hid_copies.append(
            remote(hid_in.at[pl.ds(s * PIECE, PIECE), :], hid.at[slab], slab_device(d))
        )
        hid_copies[-1].start()
    halos = [
        remote(cot_in.at[PIX - COLS : PIX, :], cot.at[0:COLS, :], slab_device(1)),
        remote(cot_in.at[0:COLS, :], cot.at[COLS + PIX : EXT, :], slab_device(7)),
        remote(pix_in.at[PIX - COLS : PIX, :], pix.at[0:COLS, :], slab_device(1)),
        remote(pix_in.at[0:COLS, :], pix.at[COLS + PIX : EXT, :], slab_device(7)),
    ]
    for copy in halos:
        copy.start()
    wq_rows = pl.ds(slab * 64, 64)
    wo_rows = pl.ds(slab * 32, 32)
    w_copies = [
        remote(wq_in.at[wq_rows, :], wq.at[chan, wq_rows, :], peer_chan),
        remote(wo_in.at[wo_rows, :], wo.at[chan, wo_rows, :], peer_chan),
    ]
    for copy in w_copies:
        copy.start()

    top = (slab > 0).astype(F32)
    bottom = (slab < 7).astype(F32)

    ld_cot.wait()
    halos[0].wait()
    halos[1].wait()

    def put_cot(b, value):
        cot3[b] = value

    wide = jnp.concatenate(
        [
            cot[0:COLS, :].astype(F32) * top,
            cot[COLS : COLS + PIX, :].astype(F32),
            cot[COLS + PIX : EXT, :].astype(F32) * bottom,
        ],
        axis=0,
    )
    shifted_columns(wide, put_cot)
    ld_wc.wait()

    def grad_half(which, m):
        total = None
        for a in range(3):
            for b in range(3):
                tap = 3 * a + b
                left = cot3[2 - b, pl.ds(pl.multiple_of((2 - a) * COLS + m * STEP, COLS), STEP), :]
                rows = pl.ds(pl.multiple_of(tap * CH + which * HALF, HALF), HALF)
                term = dot_nt(left, wc[rows, :])
                total = term if total is None else total + term
        return total

    @pl.loop(0, PIX // STEP)
    def _(m):
        rows = pl.ds(pl.multiple_of(m * STEP, STEP), STEP)
        gact_send[rows, :] = grad_half(other, m).astype(BF16)

    ld_hid.wait()
    for copy in hid_copies:
        copy.wait()
    ld_wk.wait()
    ld_wv.wait()
    squares = None
    for s in range(8):
        part = hid[s].astype(F32)
        part = jnp.sum(part * part, axis=-1, keepdims=True)
        squares = part if squares is None else squares + part
    scale = lax.rsqrt(squares / 4096.0 + 1e-06)
    key_sum, value_sum = None, None
    for s in range(8):
        context = (hid[s].astype(F32) * scale * small[s : s + 1, :]).astype(BF16)
        key_part = dot(context, wk[s * CH : (s + 1) * CH, :])
        value_part = dot(context, wv[s * CH : (s + 1) * CH, :])
        key_sum = key_part if key_sum is None else key_sum + key_part
        value_sum = value_part if value_sum is None else value_sum + value_part
    own_tokens = pl.ds(pl.multiple_of(slab * PIECE, PIECE), PIECE)
    kv[chan, own_tokens, 0:HALF] = key_sum.astype(BF16)
    kv[chan, own_tokens, HALF:CH] = value_sum.astype(BF16)
    kv_cross = remote(kv.at[chan, own_tokens, :], kv.at[chan, own_tokens, :], peer_chan)
    kv_cross.start()
    kv_copies = []
    for d in range(1, 8):
        kv_copies.append(
            remote(kv.at[chan, own_tokens, :], kv.at[chan, own_tokens, :], slab_device(d))
        )
        kv_copies[-1].start()
    gact_cross = remote(gact_send, gact_recv, peer_chan)
    gact_cross.start()

    w_spread = []
    for copy in w_copies:
        copy.wait()
    for d in range(1, 8):
        w_spread.append(
            remote(wq.at[other, wq_rows, :], wq.at[other, wq_rows, :], slab_device(d))
        )
        w_spread[-1].start()
        w_spread.append(
            remote(wo.at[other, wo_rows, :], wo.at[other, wo_rows, :], slab_device(d))
        )
        w_spread[-1].start()

    @pl.loop(0, PIX // STEP)
    def _(m):
        rows = pl.ds(pl.multiple_of(m * STEP, STEP), STEP)
        gact_own[rows, :] = grad_half(chan, m)

    ld_wt.wait()
    time_row = jnp.broadcast_to(small[9:10, :], (16, CH)).astype(BF16)
    film_rows = dot(time_row, wt[...])
    for h in range(2):
        film[h, 0] = film_rows[0:8, h * HALF : (h + 1) * HALF]
        film[h, 1] = film_rows[0:8, CH + h * HALF : CH + (h + 1) * HALF]

    kv_cross.wait()
    kv_spread = []
    for d in range(1, 8):
        kv_spread.append(
            remote(kv.at[other, own_tokens, :], kv.at[other, own_tokens, :], slab_device(d))
        )
        kv_spread[-1].start()

    ld_pix.wait()
    ld_wq.wait()
    ld_wo.wait()
    halos[2].wait()
    halos[3].wait()
    for copy in kv_copies:
        copy.wait()
    lane = lax.broadcasted_iota(jnp.int32, (TOK, STEP), 1)
    low_lanes = lane < 64
    live = lax.broadcasted_iota(jnp.int32, (STEP, TOK), 1) < lengths[0]
    zero = jnp.zeros((TOK, STEP), BF16)

    def attend(group):
        @pl.loop(0, EXT // STEP)
        def _(m):
            rows = pl.ds(pl.multiple_of(m * STEP, STEP), STEP)
            part = pix[rows, :].astype(F32)
            mean = jnp.sum(part * part, axis=-1, keepdims=True) / 512.0
            normed = (part * lax.rsqrt(mean + 1e-06) * small[8:9, :]).astype(BF16)
            query = dot(normed, wq[group]).astype(BF16)
            for pair in range(2):
                at = pair * STEP
                keys = kv[group, :, at : at + STEP]
                values = kv[group, :, HALF + at : HALF + at + STEP]
                total = None
                for head in range(2):
                    keep = low_lanes if head == 0 else jnp.logical_not(low_lanes)
                    scores = dot_nt(query[:, at : at + STEP], jnp.where(keep, keys, zero)) * 0.125
                    scores = jnp.where(live, scores, -1e30)
                    peak = jnp.max(scores, axis=-1, keepdims=True)
                    raised = jnp.exp(scores - peak)
                    soft = raised / jnp.sum(raised, axis=-1, keepdims=True)
                    term = dot(soft.astype(BF16), jnp.where(keep, values, zero))
                    total = term if total is None else total + term
                att[group, rows, at : at + STEP] = total.astype(BF16)

    attend(chan)
    for copy in w_spread:
        copy.wait()
    for copy in kv_spread:
        copy.wait()
    attend(other)

    @pl.loop(0, EXT // STEP)
    def _(m):
        rows = pl.ds(pl.multiple_of(m * STEP, STEP), STEP)
        mixed = pix[rows, :].astype(F32) + dot(att[0, rows, :], wo[0]) + dot(att[1, rows, :], wo[1])
        mix[0, rows, :] = mixed[:, 0:HALF]
        mix[1, rows, :] = mixed[:, HALF:CH]

    for h in range(2):
        lifted = mix[h] * (1.0 + film[h, 0, 0:1, :]) + film[h, 1, 0:1, :]
        active = lifted * silu_gate(lifted)
        active = jnp.concatenate(
            [active[0:COLS] * top, active[COLS : COLS + PIX], active[COLS + PIX : EXT] * bottom],
            axis=0,
        )

        def put_act(b, value):
            act3[b, :, h * HALF : (h + 1) * HALF] = value

        shifted_columns(active.astype(BF16).astype(F32), put_act)

    for tap in range(9):
        a, b = divmod(tap, 3)
        term = dot_tn(act3[b, a * COLS : a * COLS + PIX, :], cot[COLS : COLS + PIX, :])
        for block, inside, row, size in block_rows(tap):
            for h in range(2):
                cv[h, place_of(h, block), inside : inside + size, :] = term[
                    row : row + size, h * STEP : (h + 1) * STEP
                ]

    gact_cross.wait()

    @pl.loop(0, PIX // STEP)
    def _(m):
        rows = pl.ds(pl.multiple_of(m * STEP, STEP), STEP)
        rows_ext = pl.ds(pl.multiple_of(m * STEP + COLS, COLS), STEP)
        gain = 1.0 + film[chan, 0, 0:1, :]
        lifted = mix[chan, rows_ext, :] * gain + film[chan, 1, 0:1, :]
        gate = silu_gate(lifted)
        grad_act = gact_own[rows, :] + gact_recv[rows, :].astype(F32)
        grad_lift = grad_act * gate * (1.0 + lifted * (1.0 - gate))
        gact_own[rows, :] = cot[rows_ext, :].astype(F32) + grad_lift * gain

    grad_mixed = gact_own[...].astype(BF16)
    for to in range(2):
        term = dot_tn(grad_mixed, att[to, COLS : COLS + PIX, :])
        for low in range(2):
            for zz in range(4):
                for yy in range(4):
                    row = low * 128 + zz * 32 + yy * 8
                    block = (2 * (1 - to) + low) * 16 + zz * 4 + yy
                    for h in range(2):
                        cv[h, place_of(h, block), 72:80, :] = term[
                            row : row + 8, h * STEP : (h + 1) * STEP
                        ]

    @pl.loop(0, 64)
    def _(i):
        core_send[i] = cv[1 - core, i].astype(BF16)

    to_core = remote(core_send, core_recv, peer_core)
    to_core.start()

    @pl.loop(0, PIX // STEP)
    def _(m):
        rows = pl.ds(pl.multiple_of(m * STEP, STEP), STEP)
        rows_ext = pl.ds(pl.multiple_of(m * STEP + COLS, COLS), STEP)
        total = mix[chan, rows_ext, :]
        for a in range(3):
            for b in range(3):
                tap = 3 * a + b
                left = act3[b, pl.ds(pl.multiple_of(a * COLS + m * STEP, COLS), STEP), :]
                total = total + dot(left, wc[tap * CH : (tap + 1) * CH, :])
        result[rows, :] = total.astype(BF16)

    put_result = pltpu.make_async_copy(result, res_out, load_sem.at[len(loads)])
    put_result.start()

    to_core.wait()

    def summed(n, at):
        return cv[core, at + n] + core_recv[at + n].astype(F32)

    first = []
    for d in range(1, 4):
        at = lax.rem(u + d, 4) * 16

        @pl.loop(0, 16)
        def _(n):
            s1[d - 1, n] = summed(n, at).astype(BF16)

        first.append(remote(s1.at[d - 1], r1.at[d - 1], first_device(d)))
        first[-1].start()

    @pl.loop(0, 16)
    def _(n):
        a1[n] = summed(n, u * 16)

    for copy in first:
        copy.wait()

    def second_sum(n):
        return a1[n] + r1[0, n].astype(F32) + r1[1, n].astype(F32) + r1[2, n].astype(F32)

    second = []
    for d in range(1, 4):
        at = lax.rem(v + d, 4) * 4
        for n in range(4):
            s2[d - 1, n] = second_sum(at + n).astype(BF16)
        second.append(remote(s2.at[d - 1], r2.at[d - 1], second_device(d)))
        second[-1].start()
    for n in range(4):
        a2[n] = second_sum(v * 4 + n)
    for copy in second:
        copy.wait()

    def third_sum(n):
        return a2[n] + r2[0, n].astype(F32) + r2[1, n].astype(F32) + r2[2, n].astype(F32)

    third = []
    for d in range(1, 4):
        s3[d - 1] = third_sum(lax.rem(z + d, 4)).astype(BF16)
        third.append(remote(s3.at[d - 1], r3.at[d - 1], depth_device(d)))
        third[-1].start()
    own = third_sum(z)
    for copy in third:
        copy.wait()
    own = own + r3[0].astype(F32) + r3[1].astype(F32) + r3[2].astype(F32)
    a3[...] = own
    last = []
    base = count[0]
    count[0] += 2
    for k in range(2):
        last.append(
            pltpu.make_async_remote_copy(
                src_ref=a3.at[72:80],
                dst_ref=out_peer.at[core],
                send_sem=send_sem.at[base + k],
                recv_sem=recv_sem.at[base + core],
                device_id=dest[k],
                device_id_type=MESH,
            )
        )
        last[-1].start()
    conv_cross = remote(a3, conv_peer, peer_core)
    conv_cross.start()
    conv_cross.wait()
    peer = conv_peer[...]
    first_core = core == 0
    low_half = jnp.where(first_core, own, peer)
    high_half = jnp.where(first_core, peer, own)
    gconv_out[:, 0:STEP] = jnp.where(first_core, low_half[0:36], low_half[36:72])
    gconv_out[:, STEP:HALF] = jnp.where(first_core, high_half[0:36], high_half[36:72])
    for copy in last:
        copy.wait_send()
    for k in range(2):
        pltpu.make_async_remote_copy(
            src_ref=a3.at[72:80],
            dst_ref=out_peer.at[k],
            send_sem=send_sem.at[base + k],
            recv_sem=recv_sem.at[base + k],
            device_id=source[k],
            device_id_type=MESH,
        ).wait_recv()
        gout_out[:, k * STEP : (k + 1) * STEP] = jnp.where(
            first_core, out_peer[k, 0:4], out_peer[k, 4:8]
        )
    put_result.wait()


COPIES = 56
VMEM = pltpu.VMEM
ANY = pl.BlockSpec(memory_space=pl.ANY)
INSIDE = pl.BlockSpec(memory_space=pltpu.VMEM)


def time_embed(time_steps, emb_width):
    half_width = emb_width // 2
    frequency = jnp.exp(
        -math.log(10000.0) * jnp.arange(half_width).astype(F32) / half_width
    )
    angles = time_steps.astype(F32)[:, None] * frequency[None, :]
    return jnp.concatenate([jnp.sin(angles), jnp.cos(angles)], axis=1).astype(BF16)


def shards(
    pixels,
    hidden,
    enc_gain,
    lengths,
    time_steps,
    attn_gain,
    w_query,
    w_key,
    w_value,
    w_out,
    w_time,
    w_conv,
    cotangent,
):
    small = jnp.concatenate(
        [
            enc_gain.astype(F32).reshape(8, CH),
            attn_gain.astype(F32).reshape(1, CH),
            time_embed(time_steps, TEMB).astype(F32),
        ],
        axis=0,
    )
    result, grad_conv, grad_out_t = pl.pallas_call(
        kernel,
        out_shape=(
            jax.ShapeDtypeStruct((PIX, HALF), BF16),
            jax.ShapeDtypeStruct((36, HALF), F32),
            jax.ShapeDtypeStruct((4, HALF), F32),
        ),
        in_specs=[
            pl.BlockSpec(memory_space=pltpu.SMEM),
            ANY,
            ANY,
            INSIDE,
            ANY,
            ANY,
            ANY,
            ANY,
            ANY,
            ANY,
            ANY,
        ],
        out_specs=(ANY, INSIDE, INSIDE),
        scratch_shapes=[
            VMEM((EXT, CH), BF16),
            VMEM((EXT, HALF), BF16),
            VMEM((8, PIECE, CH), BF16),
            VMEM((2, CH, HALF), BF16),
            VMEM((4096, HALF), BF16),
            VMEM((4096, HALF), BF16),
            VMEM((2, HALF, CH), BF16),
            VMEM((TEMB, 2 * CH), BF16),
            VMEM((9 * CH, HALF), BF16),
            VMEM((2, TOK, CH), BF16),
            VMEM((2, 2, 8, HALF), F32),
            VMEM((2, EXT, HALF), BF16),
            VMEM((2, EXT, HALF), F32),
            VMEM((3, EXT, CH), BF16),
            VMEM((3, EXT, HALF), BF16),
            VMEM((PIX, HALF), BF16),
            VMEM((PIX, HALF), BF16),
            VMEM((PIX, HALF), F32),
            VMEM((PIX, HALF), BF16),
            VMEM((2, 64, 80, STEP), F32),
            VMEM((64, 80, STEP), BF16),
            VMEM((64, 80, STEP), BF16),
            VMEM((3, 16, 80, STEP), BF16),
            VMEM((3, 16, 80, STEP), BF16),
            VMEM((16, 80, STEP), F32),
            VMEM((3, 4, 80, STEP), BF16),
            VMEM((3, 4, 80, STEP), BF16),
            VMEM((4, 80, STEP), F32),
            VMEM((3, 80, STEP), BF16),
            VMEM((3, 80, STEP), BF16),
            VMEM((80, STEP), F32),
            VMEM((80, STEP), F32),
            VMEM((2, 8, STEP), F32),
            pltpu.SemaphoreType.DMA((10,)),
            pltpu.SemaphoreType.DMA((COPIES,)),
            pltpu.SemaphoreType.DMA((COPIES,)),
        ],
        compiler_params=pltpu.CompilerParams(
            collective_id=0, has_side_effects=True, vmem_limit_bytes=60 * 1024 * 1024
        ),
        name="block",
    )(
        lengths,
        pixels.reshape(PIX, CH),
        hidden.reshape(TOK, CH),
        small,
        w_query,
        w_key,
        w_value,
        w_out,
        w_time,
        w_conv,
        cotangent.reshape(PIX, HALF),
    )
    return result.reshape(1, ROWS, COLS, HALF), grad_conv, grad_out_t


def solution(mesh):
    finer = Mesh(
        mesh.devices.reshape(4, 4, 4, 2, mesh.shape["chan"]),
        ("dp_0", "dp_1", "space_0", "space_1", "chan"),
    )
    placed = (
        P(DP, SPACE, None, None),
        P(DP, None, SPACE),
        P(),
        P(DP),
        P(DP),
        P(),
        P(None, "chan"),
        P(None, "chan"),
        P(None, "chan"),
        P("chan", None),
        P(),
        P(None, "chan"),
        P(DP, SPACE, None, "chan"),
    )
    return jax.shard_map(
        shards,
        mesh=finer,
        in_specs=placed,
        out_specs=(P(DP, SPACE, None, "chan"), P(DP_SPACE, "chan"), P(DP_SPACE, "chan")),
        check_vma=False,
    )
```

time: 208 us -> 72.8 us (0.35)
  Pallas kernels: 0 us -> 64.1 us
  starting transfers between devices: 59.9 us -> 0 us
  waiting for transfers between devices: 59.7 us -> 0 us
  local copies, waits for them, and re-layouts: 32.4 us -> 5.75 us
  other arithmetic: 21.3 us -> 0.67 us
  matrix products: 20.3 us -> 0 us
  blocking collectives: 10.3 us -> 0 us
    pallas_call x0 -> x1, Pallas kernels: none -> 64.1 us  [shards(): pl.pallas_call(kernel, out_shape=(jax.ShapeDtypeStruct((PIX, HALF), BF16)...]
    all_to_all x6 -> x0, waiting for transfers between devices: 59.7 us -> none  [the longest x2 30.4 us: sum_in_two_steps(): lax.all_to_all(nearer.astype(jnp.bfloat16), far, split_axis=0, concat_axi...]
    all_to_all x6 -> x0, starting transfers between devices: 46 us -> none  [the longest x2 23.2 us: sum_in_two_steps(): lax.all_to_all(nearer.astype(jnp.bfloat16), far, split_axis=0, concat_axi...]
    dot_general x11 -> x0, matrix products: 19.8 us -> none  [the longest x1 5.18 us: shards(): conv_out = jnp.dot(patches, w_conv, preferred_element_type=jnp.float32)]
    ppermute x4 -> x0, starting transfers between devices: 13.9 us -> none  [the longest x2 10.1 us: padded_2(): lax.ppermute(tail, axis, [(i, (i + 1) % count) for i in range(ends)])]
    reduce_sum x8 -> x0, other arithmetic: 12 us -> none  [the longest x2 4.4 us: sum_at_owner(): return arrived.astype(jnp.float32).sum(axis=0)]
    all_to_all x2 -> x0, blocking collectives: 10.3 us -> none  [sum_at_owner(): lax.all_to_all(tiles, axis, split_axis=0, concat_axis=0, tiled=True)]
    convert_element_type x8 -> x0, other arithmetic: 8.32 us -> none  [the longest x1 2.59 us: shards(): (cot_full.astype(jnp.float32) + grad_lift * (1.0 + film_scale)).astype(jn...]
  transfers between devices with their start and end apart: 10 -> 0, of which waited for: 4 -> 0; matrix products, arithmetic and copies ran while one was open for 24% -> 0% of each run, Pallas kernels for 0% -> 0%
where the time goes in v1:
time: 72.8 us; the launch traced here: 72.4 us
  Pallas kernels  64.1 us (88%)
  local copies, waits for them, and re-layouts  5.75 us (8%)
  between operations  1.95 us (3%)
    pallas_call x1, Pallas kernels, shards(): pl.pallas_call(kernel, out_shape=(jax.ShapeDtypeStruct((PIX, HALF), BF16)...  64.1 us
    unnamed x3, local copies, waits for them, and re-layouts  4.34 us

profile of v1, /device:TPU:1, one launch (start us, length us, event | category | flops | bytes accessed | tf_op | source)
XLA Modules:
  0.0 72.4 jit_solution(12910046993556026270)
XLA Ops:
  2.0 0.7 reshape.69
  2.7 0.7 reshape.68
  3.4 0.6 maximum_convert_fusion.small
  4.0 64.1 %block.1 = (bf16[512,256]{1,0:T(8,128)(2,1)}, f32[36,256]{1,0:T(8,128)}, f32[4,256]{1,0:T(4,128)}) custom-call(s32[1]{0:T(128)S(6)} %copy.19.lengths, bf16[512,512]{1,0:T(8,128)(2,1)} %bitcast.5, bf16[128,512]{1,0:T(8,128)(2,1)} %bitcast.8, f32[10,512]{1,0:T(8,128)} %maximum_convert_fusion.small, bf16[512,256]{1,0:T(8,128)(2,1)} %wq_in.1, ...), custom_call_target="tpu_custom_call" | custom-call | tf_op jit(solution)/shard_map/block/pallas_call | solution.py:576
  68.1 1.7 %copy.21 = bf16[1,8,64,256]{3,2,1,0:T(8,128)(2,1)} copy(bf16[1,8,64,256]{3,2,1,0:T(8,128)(2,1)} %bitcast.7) | data formatting | bytes 524288
  69.8 1.4 %copy.22 = f32[36,256]{1,0:T(8,128)} copy(f32[36,256]{1,0:T(8,128)} %get-tuple-element.15) | data formatting | bytes 73728
  71.2 1.3 %copy.23 = f32[4,256]{1,0:T(4,128)} copy(f32[4,256]{1,0:T(4,128)} %get-tuple-element.16) | data formatting | bytes 8192
  (3 shorter events, 0.1 us)

commit v2 on v1

v2 whole, which is shorter than its diff:
```python
import math

import jax
import jax.numpy as jnp
from jax import lax
from jax.experimental import pallas as pl
from jax.experimental.pallas import tpu as pltpu
from jax.sharding import Mesh
from jax.sharding import PartitionSpec as P

TEMB = 512
SPACE = ("space_0", "space_1")
DP_SPACE = ("dp_0", "dp_1", "space_0", "space_1")
DP = ("dp_0", "dp_1")
F32 = jnp.float32
BF16 = jnp.bfloat16
MESH = pl.DeviceIdType.MESH

ROWS = 8
COLS = 64
PIX = ROWS * COLS
EXT = PIX + 2 * COLS
CH = 512
HALF = 256
TOK = 128
PIECE = 16
STEP = 128


def dot(a, b):
    return jnp.dot(a, b, preferred_element_type=F32)


def dot_nt(a, b):
    return lax.dot_general(a, b, (((1,), (1,)), ((), ())), preferred_element_type=F32)


def dot_tn(a, b):
    return lax.dot_general(a, b, (((0,), (0,)), ((), ())), preferred_element_type=F32)


def silu_gate(lifted):
    return 1.0 / (1.0 + jnp.exp(-lifted))


def shifted_columns(wide, store):
    col = lax.rem(lax.broadcasted_iota(jnp.int32, wide.shape, 0), COLS)
    down = pltpu.roll(wide, 1, 0)
    up = pltpu.roll(wide, wide.shape[0] - 1, 0)
    store(0, jnp.where(col == 0, 0.0, down).astype(BF16))
    store(1, wide.astype(BF16))
    store(2, jnp.where(col == COLS - 1, 0.0, up).astype(BF16))


def block_rows(tap):
    pieces = []
    row = tap * CH
    while row < (tap + 1) * CH:
        block, inside = divmod(row, 72)
        count = min(72 - inside, (tap + 1) * CH - row)
        pieces.append((block, inside, row - tap * CH, count))
        row += count
    return pieces


def place_of(half, block):
    x, z, y = block // 16, (block // 4) % 4, block % 4
    u, v = (x, y) if half == 0 else (y, x)
    return (z // 2) * 32 + u * 8 + v * 2 + z % 2


def whole_place(half, block):
    x, z, y = block // 16, (block // 4) % 4, block % 4
    u, v = (x, y) if half == 0 else (y, x)
    return u * 16 + v * 4 + z


def kernel(
    lengths,
    pix_in,
    hid_in,
    enc_in,
    attn_in,
    time_in,
    wq_in,
    wk_in,
    wv_in,
    wo_in,
    wt_in,
    wc_in,
    cot_in,
    res_out,
    gconv_out,
    gout_out,
    pix,
    cot,
    hid_own,
    hid,
    wq,
    wk,
    wv,
    wo,
    wt,
    wc,
    kv,
    film,
    normed,
    query,
    att,
    mix,
    act3,
    cot3,
    gact_send,
    gact_recv,
    gact_own,
    gmix,
    result,
    cv,
    core_send,
    core_recv,
    s1,
    r1,
    a1,
    s2,
    r2,
    a2,
    s3,
    r3,
    a3,
    conv_peer,
    ov,
    core_send_o,
    core_recv_o,
    s1o,
    r1o,
    a1o,
    s2o,
    r2o,
    a2o,
    s3o,
    r3o,
    a3o,
    out_peer,
    load_sem,
    send_sem,
    recv_sem,
):
    x = lax.axis_index("dp_0")
    z = lax.axis_index("dp_1")
    y = lax.axis_index("space_0")
    core = lax.axis_index("space_1")
    chan = lax.axis_index("chan")
    other = 1 - chan
    slab = y * 2 + core
    piece = x * 2 + core
    count = [0]

    def remote(src, dst, device):
        i = count[0]
        count[0] += 1
        return pltpu.make_async_remote_copy(
            src_ref=src,
            dst_ref=dst,
            send_sem=send_sem.at[i],
            recv_sem=recv_sem.at[i],
            device_id=device,
            device_id_type=MESH,
        )

    def slab_device(d):
        s = lax.rem(slab + d, 8)
        return {"space_0": s // 2, "space_1": lax.rem(s, 2)}

    u = x * (1 - core) + y * core
    v = y * (1 - core) + x * core

    def first_device(d):
        t = lax.rem(u + d, 4)
        return {"dp_0": t * (1 - core) + x * core, "space_0": y * (1 - core) + t * core}

    def second_device(d):
        t = lax.rem(v + d, 4)
        return {"dp_0": x * (1 - core) + t * core, "space_0": t * (1 - core) + y * core}

    def depth_device(d):
        return {"dp_1": lax.rem(z + d, 4)}

    peer_chan = {"chan": other}
    peer_core = {"space_1": 1 - core}
    half_x, low_x = x // 2, lax.rem(x, 2)
    dest = [{"dp_0": 2 * chan + low_x, "space_1": k, "chan": 1 - half_x} for k in range(2)]
    source = [{"dp_0": 2 * (1 - chan) + low_x, "space_1": k, "chan": half_x} for k in range(2)]

    def piece_device(d):
        p = lax.rem(piece + d, 8)
        return {"dp_0": p // 2, "space_1": lax.rem(p, 2)}

    barrier = pltpu.get_barrier_semaphore()
    greeted = (
        [peer_chan]
        + dest
        + source
        + [depth_device(d) for d in range(1, 4)]
        + [piece_device(d) for d in range(1, 8)]
        + [slab_device(d) for d in range(1, 8)]
    )
    for device in greeted:
        pl.semaphore_signal(barrier, inc=1, device_id=device, device_id_type=MESH)

    loads = []

    def load(src, dst):
        copy = pltpu.make_async_copy(src, dst, load_sem.at[len(loads)])
        copy.start()
        loads.append(copy)
        return copy

    ld_hid = load(hid_in, hid_own)
    ld_pix = load(pix_in, pix.at[COLS : COLS + PIX, :])
    ld_wq = load(wq_in, wq.at[chan])
    ld_cot = load(cot_in, cot.at[COLS : COLS + PIX, :])
    ld_wc = load(wc_in, wc)
    ld_wk = load(wk_in, wk)
    ld_wv = load(wv_in, wv)
    ld_wo = load(wo_in, wo.at[chan])
    ld_wt = load(wt_in, wt)

    top = (slab > 0).astype(F32)
    bottom = (slab < 7).astype(F32)
    attn = attn_in[...].astype(F32)
    attn_row = jnp.concatenate([attn[i : i + 1, :] for i in range(4)], axis=1)

    def query_rows(rows):
        part = pix[rows, :].astype(F32)
        mean = jnp.sum(part * part, axis=-1, keepdims=True) / 512.0
        norm = (part * lax.rsqrt(mean + 1e-06) * attn_row).astype(BF16)
        normed[rows, :] = norm
        query[chan, rows, :] = dot(norm, wq[chan]).astype(BF16)

    ld_pix.wait()
    ld_wq.wait()

    @pl.loop(0, PIX // STEP)
    def _(m):
        query_rows(pl.ds(pl.multiple_of(m * STEP + COLS, COLS), STEP))

    ld_hid.wait()
    ld_cot.wait()
    pl.semaphore_wait(barrier, len(greeted))

    hid_copies = []
    for d in range(1, 8):
        s = lax.rem(slab + d, 8)
        there = pl.ds(pl.multiple_of(s * PIECE, PIECE), PIECE)
        hid_copies.append(remote(hid_own.at[there, :], hid.at[slab], slab_device(d)))
        hid_copies[-1].start()
    wq_rows = pl.ds(pl.multiple_of(piece * 64, 64), 64)
    wo_rows = pl.ds(pl.multiple_of(piece * 32, 32), 32)
    w_copies = [
        remote(wq_in.at[wq_rows, :], wq.at[chan, wq_rows, :], peer_chan),
        remote(wo_in.at[wo_rows, :], wo.at[chan, wo_rows, :], peer_chan),
    ]
    for copy in w_copies:
        copy.start()
    halos = [
        remote(pix.at[PIX : PIX + COLS, :], pix.at[0:COLS, :], slab_device(1)),
        remote(pix.at[COLS : 2 * COLS, :], pix.at[COLS + PIX : EXT, :], slab_device(7)),
        remote(cot.at[PIX : PIX + COLS, :], cot.at[0:COLS, :], slab_device(1)),
        remote(cot.at[COLS : 2 * COLS, :], cot.at[COLS + PIX : EXT, :], slab_device(7)),
    ]
    for copy in halos:
        copy.start()

    def shift_cot(start, size, factor):
        wide = cot[start : start + size, :].astype(F32)
        if factor is not None:
            wide = wide * factor

        def put_cot(b, value):
            cot3[b, start : start + size, :] = value

        shifted_columns(wide, put_cot)

    shift_cot(COLS, PIX, None)
    ld_wc.wait()

    def grad_half(which, m):
        total = None
        for a in range(3):
            for b in range(3):
                tap = 3 * a + b
                left = cot3[2 - b, pl.ds(pl.multiple_of((2 - a) * COLS + m * STEP, COLS), STEP), :]
                rows = pl.ds(pl.multiple_of(tap * CH + which * HALF, HALF), HALF)
                term = dot_nt(left, wc[rows, :])
                total = term if total is None else total + term
        return total

    def grad_rows(m):
        rows = pl.ds(pl.multiple_of(m * STEP, STEP), STEP)
        gact_send[rows, :] = grad_half(other, m).astype(BF16)
        gact_own[rows, :] = grad_half(chan, m)

    @pl.loop(1, 3)
    def _(m):
        grad_rows(m)

    gact_inner = remote(
        gact_send.at[STEP : 3 * STEP, :], gact_recv.at[STEP : 3 * STEP, :], peer_chan
    )

    enc = enc_in[...].astype(F32)
    ld_wk.wait()
    ld_wv.wait()
    for copy in hid_copies:
        copy.wait()
    own_tokens = pl.ds(pl.multiple_of(slab * PIECE, PIECE), PIECE)
    hid[slab] = hid_own[own_tokens, :]
    squares = None
    for s in range(8):
        part = hid[s].astype(F32)
        part = jnp.sum(part * part, axis=-1, keepdims=True)
        squares = part if squares is None else squares + part
    scale = lax.rsqrt(squares / 4096.0 + 1e-06)
    key_sum, value_sum = None, None
    for s in range(8):
        gain = jnp.concatenate([enc[4 * s + i : 4 * s + i + 1, :] for i in range(4)], axis=1)
        context = (hid[s].astype(F32) * scale * gain).astype(BF16)
        key_part = dot(context, wk[s * CH : (s + 1) * CH, :])
        value_part = dot(context, wv[s * CH : (s + 1) * CH, :])
        key_sum = key_part if key_sum is None else key_sum + key_part
        value_sum = value_part if value_sum is None else value_sum + value_part
    kv[chan, own_tokens, 0:HALF] = key_sum.astype(BF16)
    kv[chan, own_tokens, HALF:CH] = value_sum.astype(BF16)
    kv_cross = remote(kv.at[chan, own_tokens, :], kv.at[chan, own_tokens, :], peer_chan)
    kv_cross.start()
    kv_copies = []
    for d in range(1, 8):
        kv_copies.append(
            remote(kv.at[chan, own_tokens, :], kv.at[chan, own_tokens, :], slab_device(d))
        )
        kv_copies[-1].start()
    gact_inner.start()

    w_spread = []
    for copy in w_copies:
        copy.wait()
    for d in range(1, 8):
        w_spread.append(
            remote(wq.at[other, wq_rows, :], wq.at[other, wq_rows, :], piece_device(d))
        )
        w_spread[-1].start()
    for d in range(1, 8):
        w_spread.append(
            remote(wo.at[other, wo_rows, :], wo.at[other, wo_rows, :], piece_device(d))
        )
        w_spread[-1].start()

    for copy in halos:
        copy.wait()
    query_rows(pl.ds(0, COLS))
    query_rows(pl.ds(COLS + PIX, COLS))
    shift_cot(0, COLS, top)
    shift_cot(COLS + PIX, COLS, bottom)

    @pl.loop(0, 2)
    def _(m):
        grad_rows(m * 3)

    gact_edges = [
        remote(gact_send.at[at : at + STEP, :], gact_recv.at[at : at + STEP, :], peer_chan)
        for at in (0, 3 * STEP)
    ]
    for copy in gact_edges:
        copy.start()

    kv_cross.wait()
    kv_spread = []
    for d in range(1, 8):
        kv_spread.append(
            remote(kv.at[other, own_tokens, :], kv.at[other, own_tokens, :], slab_device(d))
        )
        kv_spread[-1].start()

    ld_wt.wait()
    time_row = jnp.broadcast_to(time_in[...].astype(F32), (16, CH)).astype(BF16)
    film_rows = dot(time_row, wt[...])
    for h in range(2):
        film[h, 0] = film_rows[0:8, h * HALF : (h + 1) * HALF]
        film[h, 1] = film_rows[0:8, CH + h * HALF : CH + (h + 1) * HALF]

    ld_wo.wait()
    for copy in kv_copies:
        copy.wait()
    lane = lax.broadcasted_iota(jnp.int32, (TOK, STEP), 1)
    low_lanes = lane < 64
    live = lax.broadcasted_iota(jnp.int32, (STEP, TOK), 1) < lengths[0]
    zero = jnp.zeros((TOK, STEP), BF16)

    def attend(group, rows):
        for pair in range(2):
            at = pair * STEP
            keys = kv[group, :, at : at + STEP]
            values = kv[group, :, HALF + at : HALF + at + STEP]
            total = None
            for head in range(2):
                keep = low_lanes if head == 0 else jnp.logical_not(low_lanes)
                scores = dot_nt(query[group, rows, at : at + STEP], jnp.where(keep, keys, zero))
                scores = jnp.where(live, scores * 0.125, -1e30)
                peak = jnp.max(scores, axis=-1, keepdims=True)
                raised = jnp.exp(scores - peak)
                soft = raised / jnp.sum(raised, axis=-1, keepdims=True)
                term = dot(soft.astype(BF16), jnp.where(keep, values, zero))
                total = term if total is None else total + term
            att[group, rows, at : at + STEP] = total.astype(BF16)

    @pl.loop(0, EXT // STEP)
    def _(m):
        rows = pl.ds(pl.multiple_of(m * STEP, STEP), STEP)
        attend(chan, rows)
        mixed = pix[rows, :].astype(F32) + dot(att[chan, rows, :], wo[chan])
        mix[0, rows, :] = mixed[:, 0:HALF]
        mix[1, rows, :] = mixed[:, HALF:CH]

    for copy in w_spread:
        copy.wait()

    @pl.loop(0, EXT // STEP)
    def _(m):
        rows = pl.ds(pl.multiple_of(m * STEP, STEP), STEP)
        query[other, rows, :] = dot(normed[rows, :], wq[other]).astype(BF16)

    for copy in kv_spread:
        copy.wait()

    @pl.loop(0, EXT // STEP)
    def _(m):
        rows = pl.ds(pl.multiple_of(m * STEP, STEP), STEP)
        attend(other, rows)
        mixed = dot(att[other, rows, :], wo[other])
        mix[0, rows, :] += mixed[:, 0:HALF]
        mix[1, rows, :] += mixed[:, HALF:CH]

    for h in range(2):
        lifted = mix[h] * (1.0 + film[h, 0, 0:1, :]) + film[h, 1, 0:1, :]
        active = lifted * silu_gate(lifted)
        active = jnp.concatenate(
            [active[0:COLS] * top, active[COLS : COLS + PIX], active[COLS + PIX : EXT] * bottom],
            axis=0,
        )

        def put_act(b, value):
            act3[b, :, h * HALF : (h + 1) * HALF] = value

        shifted_columns(active.astype(BF16).astype(F32), put_act)

    for tap in range(9):
        a, b = divmod(tap, 3)
        term = dot_tn(act3[b, a * COLS : a * COLS + PIX, :], cot[COLS : COLS + PIX, :])
        for block, inside, row, size in block_rows(tap):
            for h in range(2):
                at = place_of(h, block) * 72 + inside
                cv[h, at : at + size, :] = term[row : row + size, h * STEP : (h + 1) * STEP]

    to_core = []
    for c in range(2):

        @pl.loop(0, 2304 // 144)
        def _(i):
            rows = pl.ds(pl.multiple_of(c * 2304 + i * 144, 16), 144)
            core_send[rows, :] = cv[1 - core, rows, :].astype(BF16)

        rows = slice(c * 2304, (c + 1) * 2304)
        to_core.append(remote(core_send.at[rows, :], core_recv.at[rows, :], peer_core))
        to_core[-1].start()

    gact_inner.wait()
    for copy in gact_edges:
        copy.wait()

    @pl.loop(0, PIX // STEP)
    def _(m):
        rows = pl.ds(pl.multiple_of(m * STEP, STEP), STEP)
        rows_ext = pl.ds(pl.multiple_of(m * STEP + COLS, COLS), STEP)
        gain = 1.0 + film[chan, 0, 0:1, :]
        lifted = mix[chan, rows_ext, :] * gain + film[chan, 1, 0:1, :]
        gate = silu_gate(lifted)
        grad_act = gact_own[rows, :] + gact_recv[rows, :].astype(F32)
        grad_lift = grad_act * gate * (1.0 + lifted * (1.0 - gate))
        gmix[rows, :] = (cot[rows_ext, :].astype(F32) + grad_lift * gain).astype(BF16)

    for to in range(2):
        term = dot_tn(gmix[...], att[to, COLS : COLS + PIX, :])
        for low in range(2):
            for zz in range(4):
                for yy in range(4):
                    row = low * 128 + zz * 32 + yy * 8
                    block = (2 * (1 - to) + low) * 16 + zz * 4 + yy
                    for h in range(2):
                        at = whole_place(h, block) * 8
                        ov[h, at : at + 8, :] = term[row : row + 8, h * STEP : (h + 1) * STEP]
    core_send_o[...] = ov[1 - core].astype(BF16)
    to_core_o = remote(core_send_o, core_recv_o, peer_core)
    to_core_o.start()

    first = [[], []]

    def first_stage(c):
        to_core[c].wait()
        for d in range(1, 4):
            start = c * 2304 + lax.rem(u + d, 4) * 576

            @pl.loop(0, 4)
            def _(i):
                rows = pl.ds(pl.multiple_of(start + i * 144, 16), 144)
                total = cv[core, rows, :] + core_recv[rows, :].astype(F32)
                s1[c, d - 1, pl.ds(pl.multiple_of(i * 144, 16), 144), :] = total.astype(BF16)

            first[c].append(remote(s1.at[c, d - 1], r1.at[c, d - 1], first_device(d)))
            first[c][-1].start()

    first_stage(0)
    to_core_o.wait()
    first_o = []
    for d in range(1, 4):
        rows = pl.ds(pl.multiple_of(lax.rem(u + d, 4) * 128, 128), 128)
        total = ov[core, rows, :] + core_recv_o[rows, :].astype(F32)
        s1o[d - 1] = total.astype(BF16)
        first_o.append(remote(s1o.at[d - 1], r1o.at[d - 1], first_device(d)))
        first_o[-1].start()
    first_stage(1)

    @pl.loop(0, PIX // STEP)
    def _(m):
        rows = pl.ds(pl.multiple_of(m * STEP, STEP), STEP)
        rows_ext = pl.ds(pl.multiple_of(m * STEP + COLS, COLS), STEP)
        total = mix[chan, rows_ext, :]
        for a in range(3):
            for b in range(3):
                tap = 3 * a + b
                left = act3[b, pl.ds(pl.multiple_of(a * COLS + m * STEP, COLS), STEP), :]
                total = total + dot(left, wc[tap * CH : (tap + 1) * CH, :])
        result[rows, :] = total.astype(BF16)

    put_result = pltpu.make_async_copy(result, res_out, load_sem.at[len(loads)])
    put_result.start()

    for c in range(2):

        @pl.loop(0, 4)
        def _(i):
            rows = pl.ds(pl.multiple_of(c * 2304 + u * 576 + i * 144, 16), 144)
            a1[c, pl.ds(pl.multiple_of(i * 144, 16), 144), :] = cv[core, rows, :] + core_recv[
                rows, :
            ].astype(F32)

    for copy in first_o:
        copy.wait()
    rows = pl.ds(pl.multiple_of(u * 128, 128), 128)
    a1o[...] = (
        ov[core, rows, :]
        + core_recv_o[rows, :].astype(F32)
        + r1o[0].astype(F32)
        + r1o[1].astype(F32)
        + r1o[2].astype(F32)
    )
    second_o = []
    for d in range(1, 4):
        rows = pl.ds(pl.multiple_of(lax.rem(v + d, 4) * 32, 32), 32)
        s2o[d - 1] = a1o[rows, :].astype(BF16)
        second_o.append(remote(s2o.at[d - 1], r2o.at[d - 1], second_device(d)))
        second_o[-1].start()

    second = [[], []]

    def second_stage(c):
        for copy in first[c]:
            copy.wait()

        def total(at):
            rows = pl.ds(pl.multiple_of(at * 144, 16), 144)
            return (
                a1[c, rows, :]
                + r1[c, 0, rows, :].astype(F32)
                + r1[c, 1, rows, :].astype(F32)
                + r1[c, 2, rows, :].astype(F32)
            )

        for d in range(1, 4):
            s2[c, d - 1] = total(lax.rem(v + d, 4)).astype(BF16)
            second[c].append(remote(s2.at[c, d - 1], r2.at[c, d - 1], second_device(d)))
            second[c][-1].start()
        a2[c] = total(v)

    second_stage(0)
    for copy in second_o:
        copy.wait()
    rows = pl.ds(pl.multiple_of(v * 32, 32), 32)
    a2o[...] = (
        a1o[rows, :] + r2o[0].astype(F32) + r2o[1].astype(F32) + r2o[2].astype(F32)
    )
    third_o = []
    for d in range(1, 4):
        rows = pl.ds(pl.multiple_of(lax.rem(z + d, 4) * 8, 8), 8)
        s3o[d - 1] = a2o[rows, :]
        third_o.append(remote(s3o.at[d - 1], r3o.at[d - 1], depth_device(d)))
        third_o[-1].start()
    second_stage(1)
    for copy in third_o:
        copy.wait()
    rows = pl.ds(pl.multiple_of(z * 8, 8), 8)
    a3o[...] = a2o[rows, :] + r3o[0] + r3o[1] + r3o[2]
    last = []
    base = count[0]
    count[0] += 2
    for k in range(2):
        last.append(
            pltpu.make_async_remote_copy(
                src_ref=a3o,
                dst_ref=out_peer.at[core],
                send_sem=send_sem.at[base + k],
                recv_sem=recv_sem.at[base + core],
                device_id=dest[k],
                device_id_type=MESH,
            )
        )
        last[-1].start()

    for c in range(2):
        for copy in second[c]:
            copy.wait()

    for c in range(2):
        a2[c] = (
            a2[c] + r2[c, 0].astype(F32) + r2[c, 1].astype(F32) + r2[c, 2].astype(F32)
        )

    def third_rows(t):
        rows = pl.ds(pl.multiple_of(lax.rem(t, 2) * 72, 8), 72)
        return a2[t // 2, rows, :]

    pad = jnp.zeros((8, STEP), F32)
    third = []
    for d in range(1, 4):
        total = third_rows(lax.rem(z + d, 4))
        s3[d - 1] = jnp.concatenate([total, pad], axis=0).astype(BF16)
        third.append(remote(s3.at[d - 1], r3.at[d - 1], depth_device(d)))
        third[-1].start()
    own = third_rows(z)
    for copy in third:
        copy.wait()
    arrived = r3[0].astype(F32) + r3[1].astype(F32) + r3[2].astype(F32)
    own = own + arrived[0:72]
    a3[...] = own
    conv_cross = remote(a3, conv_peer, peer_core)
    conv_cross.start()
    first_core = core == 0
    for copy in last:
        copy.wait_send()
    for k in range(2):
        pltpu.make_async_remote_copy(
            src_ref=a3o,
            dst_ref=out_peer.at[k],
            send_sem=send_sem.at[base + k],
            recv_sem=recv_sem.at[base + k],
            device_id=source[k],
            device_id_type=MESH,
        ).wait_recv()
        gout_out[:, k * STEP : (k + 1) * STEP] = jnp.where(
            first_core, out_peer[k, 0:4], out_peer[k, 4:8]
        )
    conv_cross.wait()
    peer = conv_peer[...]
    low_half = jnp.where(first_core, own, peer)
    high_half = jnp.where(first_core, peer, own)
    gconv_out[:, 0:STEP] = jnp.where(first_core, low_half[0:36], low_half[36:72])
    gconv_out[:, STEP:HALF] = jnp.where(first_core, high_half[0:36], high_half[36:72])
    put_result.wait()
    assert count[0] == COPIES


def output_kernel(a, b, c, a_out, b_out, c_out, sems):
    copies = [
        pltpu.make_async_copy(src, dst, sems.at[i])
        for i, (src, dst) in enumerate(((a, a_out), (b, b_out), (c, c_out)))
    ]
    for copy in copies:
        copy.start()
    for copy in copies:
        copy.wait()


COPIES = 75
VMEM = pltpu.VMEM
ANY = pl.BlockSpec(memory_space=pl.ANY)
INSIDE = pl.BlockSpec(memory_space=pltpu.VMEM)


def time_embed(time_steps, emb_width):
    half_width = emb_width // 2
    lane = jnp.arange(emb_width)
    place = lax.rem(lane, half_width).astype(F32)
    frequency = jnp.exp(-math.log(10000.0) * place / half_width)
    angles = time_steps.astype(F32)[:, None] * frequency[None, :]
    return jnp.where((lane < half_width)[None, :], jnp.sin(angles), jnp.cos(angles)).astype(BF16)


def shards(
    pixels,
    hidden,
    enc_gain,
    lengths,
    time_steps,
    attn_gain,
    w_query,
    w_key,
    w_value,
    w_out,
    w_time,
    w_conv,
    cotangent,
):
    time_row = time_embed(time_steps, TEMB)
    result, grad_conv, grad_out_t = pl.pallas_call(
        kernel,
        out_shape=(
            jax.ShapeDtypeStruct((PIX, HALF), BF16),
            jax.ShapeDtypeStruct((36, HALF), F32),
            jax.ShapeDtypeStruct((4, HALF), F32),
        ),
        in_specs=[
            pl.BlockSpec(memory_space=pltpu.SMEM),
            ANY,
            ANY,
            INSIDE,
            INSIDE,
            INSIDE,
            ANY,
            ANY,
            ANY,
            ANY,
            ANY,
            ANY,
            ANY,
        ],
        out_specs=(ANY, INSIDE, INSIDE),
        scratch_shapes=[
            VMEM((EXT, CH), BF16),
            VMEM((EXT, HALF), BF16),
            VMEM((TOK, CH), BF16),
            VMEM((8, PIECE, CH), BF16),
            VMEM((2, CH, HALF), BF16),
            VMEM((4096, HALF), BF16),
            VMEM((4096, HALF), BF16),
            VMEM((2, HALF, CH), BF16),
            VMEM((TEMB, 2 * CH), BF16),
            VMEM((9 * CH, HALF), BF16),
            VMEM((2, TOK, CH), BF16),
            VMEM((2, 2, 8, HALF), F32),
            VMEM((EXT, CH), BF16),
            VMEM((2, EXT, HALF), BF16),
            VMEM((2, EXT, HALF), BF16),
            VMEM((2, EXT, HALF), F32),
            VMEM((3, EXT, CH), BF16),
            VMEM((3, EXT, HALF), BF16),
            VMEM((PIX, HALF), BF16),
            VMEM((PIX, HALF), BF16),
            VMEM((PIX, HALF), F32),
            VMEM((PIX, HALF), BF16),
            VMEM((PIX, HALF), BF16),
            VMEM((2, 4608, STEP), F32),
            VMEM((4608, STEP), BF16),
            VMEM((4608, STEP), BF16),
            VMEM((2, 3, 576, STEP), BF16),
            VMEM((2, 3, 576, STEP), BF16),
            VMEM((2, 576, STEP), F32),
            VMEM((2, 3, 144, STEP), BF16),
            VMEM((2, 3, 144, STEP), BF16),
            VMEM((2, 144, STEP), F32),
            VMEM((3, 80, STEP), BF16),
            VMEM((3, 80, STEP), BF16),
            VMEM((72, STEP), F32),
            VMEM((72, STEP), F32),
            VMEM((2, 512, STEP), F32),
            VMEM((512, STEP), BF16),
            VMEM((512, STEP), BF16),
            VMEM((3, 128, STEP), BF16),
            VMEM((3, 128, STEP), BF16),
            VMEM((128, STEP), F32),
            VMEM((3, 32, STEP), BF16),
            VMEM((3, 32, STEP), BF16),
            VMEM((32, STEP), F32),
            VMEM((3, 8, STEP), F32),
            VMEM((3, 8, STEP), F32),
            VMEM((8, STEP), F32),
            VMEM((2, 8, STEP), F32),
            pltpu.SemaphoreType.DMA((10,)),
            pltpu.SemaphoreType.DMA((COPIES,)),
            pltpu.SemaphoreType.DMA((COPIES,)),
        ],
        compiler_params=pltpu.CompilerParams(
            collective_id=0, has_side_effects=True, vmem_limit_bytes=60 * 1024 * 1024
        ),
        name="block",
    )(
        lengths,
        pixels.reshape(PIX, CH),
        hidden.reshape(TOK, CH),
        enc_gain.reshape(32, STEP),
        attn_gain.reshape(4, STEP),
        time_row,
        w_query,
        w_key,
        w_value,
        w_out,
        w_time,
        w_conv,
        cotangent.reshape(PIX, HALF),
    )
    result, grad_conv, grad_out_t = pl.pallas_call(
        output_kernel,
        out_shape=(
            jax.ShapeDtypeStruct((PIX, HALF), BF16),
            jax.ShapeDtypeStruct((36, HALF), F32),
            jax.ShapeDtypeStruct((4, HALF), F32),
        ),
        in_specs=[ANY] * 3,
        out_specs=(INSIDE,) * 3,
        scratch_shapes=[pltpu.SemaphoreType.DMA((3,))],
        compiler_params=pltpu.CompilerParams(vmem_limit_bytes=60 * 1024 * 1024),
        name="outputs",
    )(result, grad_conv, grad_out_t)
    return result.reshape(1, ROWS, COLS, HALF), grad_conv, grad_out_t


def solution(mesh):
    finer = Mesh(
        mesh.devices.reshape(4, 4, 4, 2, mesh.shape["chan"]),
        ("dp_0", "dp_1", "space_0", "space_1", "chan"),
    )
    placed = (
        P(DP, SPACE, None, None),
        P(DP, None, SPACE),
        P(),
        P(DP),
        P(DP),
        P(),
        P(None, "chan"),
        P(None, "chan"),
        P(None, "chan"),
        P("chan", None),
        P(),
        P(None, "chan"),
        P(DP, SPACE, None, "chan"),
    )
    return jax.shard_map(
        shards,
        mesh=finer,
        in_specs=placed,
        out_specs=(P(DP, SPACE, None, "chan"), P(DP_SPACE, "chan"), P(DP_SPACE, "chan")),
        check_vma=False,
    )
```

time: 72.8 us -> 63.3 us (0.87)
  local copies, waits for them, and re-layouts: 5.75 us -> 0 us
  Pallas kernels: 64.1 us -> 60.5 us
    pallas_call x1, Pallas kernels: 64.1 us -> 58.8 us  [shards(): pl.pallas_call(kernel, out_shape=(jax.ShapeDtypeStruct((PIX, HALF), BF16)...]
    unnamed x3 -> x0, local copies, waits for them, and re-layouts: 4.34 us -> none
    pallas_call x0 -> x1, Pallas kernels: none -> 1.7 us  [shards(): pl.pallas_call(output_kernel, out_shape=(jax.ShapeDtypeStruct((PIX, HALF)...]
    reshape x2 -> x0, local copies, waits for them, and re-layouts: 1.4 us -> none  [the longest x1 0.71 us: shards(): enc_gain.astype(F32).reshape(8, CH)]
where the time goes in v2:
time: 63.3 us; the launch traced here: 63.1 us
  Pallas kernels  60.5 us (96%)
  between operations  1.93 us (3%)
  other arithmetic  0.67 us (1%)
    pallas_call x1, Pallas kernels, shards(): pl.pallas_call(kernel, out_shape=(jax.ShapeDtypeStruct((PIX, HALF), BF16)...  58.8 us
    pallas_call x1, Pallas kernels, shards(): pl.pallas_call(output_kernel, out_shape=(jax.ShapeDtypeStruct((PIX, HALF)...  1.7 us

profile of v2, /device:TPU:1, one launch (start us, length us, event | category | flops | bytes accessed | tf_op | source)
XLA Modules:
  0.0 63.1 jit_solution(13899656316241860407)
XLA Ops:
  1.9 0.7 %fusion.time_in = bf16[1,512]{1,0:T(2,128)(2,1)} fusion(f32[]{:T(128)} %bitcast.4), kind=kLoop, calls=%fused_computation.1 | loop fusion | flops 3584 | bytes 1028 | tf_op jit(solution)/shard_map/convert_element_type | solution.py:704
  2.6 58.8 %block.1 = (bf16[512,256]{1,0:T(8,128)(2,1)}, f32[36,256]{1,0:T(8,128)}, f32[4,256]{1,0:T(4,128)}) custom-call(s32[1]{0:T(128)S(6)} %copy.16.lengths, bf16[512,512]{1,0:T(8,128)(2,1)} %bitcast.7, bf16[128,512]{1,0:T(8,128)(2,1)} %bitcast.9, bf16[32,128]{1,0:T(8,128)(2,1)} %bitcast.10, bf16[4,128]{1,0:T(4,128)(2,1)} %bitcast.11, bf16[1,512]{1,0:T(2,128)(2,1)} %fusion.time_in, ...), custom_call_target="tpu_custom_call" | custom-call | tf_op jit(solution)/shard_map/block/pallas_call | solution.py:723
  61.4 1.7 %outputs.1 = (bf16[512,256]{1,0:T(8,128)(2,1)}, f32[36,256]{1,0:T(8,128)}, f32[4,256]{1,0:T(4,128)}) custom-call(bf16[512,256]{1,0:T(8,128)(2,1)} %get-tuple-element.9.a, f32[36,256]{1,0:T(8,128)} %get-tuple-element.10.b, f32[4,256]{1,0:T(4,128)} %get-tuple-element.11.c), custom_call_target="tpu_custom_call" | custom-call | tf_op jit(solution)/shard_map/outputs/pallas_call | solution.py:819

commit v3 on v2

--- a/solution.py
+++ b/solution.py
@@ -126,8 +126,6 @@
     a2,
     s3,
     r3,
-    a3,
-    conv_peer,
     ov,
     core_send_o,
     core_recv_o,
@@ -182,6 +180,9 @@
         t = lax.rem(v + d, 4)
         return {"dp_0": x * (1 - core) + t * core, "space_0": t * (1 - core) + y * core}
 
+    def depth_core_device(d, k):
+        return {"dp_1": lax.rem(z + d, 4), "space_1": k}
+
     def depth_device(d):
         return {"dp_1": lax.rem(z + d, 4)}
 
@@ -201,6 +202,7 @@
         + dest
         + source
         + [depth_device(d) for d in range(1, 4)]
+        + [depth_core_device(d, 1 - core) for d in range(1, 4)]
         + [piece_device(d) for d in range(1, 8)]
         + [slab_device(d) for d in range(1, 8)]
     )
@@ -311,6 +313,13 @@
     enc = enc_in[...].astype(F32)
     ld_wk.wait()
     ld_wv.wait()
+    w_spread = []
+    w_copies[0].wait()
+    for d in range(1, 8):
+        w_spread.append(
+            remote(wq.at[other, wq_rows, :], wq.at[other, wq_rows, :], piece_device(d))
+        )
+        w_spread[-1].start()
     for copy in hid_copies:
         copy.wait()
     own_tokens = pl.ds(pl.multiple_of(slab * PIECE, PIECE), PIECE)
@@ -341,14 +350,7 @@
         kv_copies[-1].start()
     gact_inner.start()
 
-    w_spread = []
-    for copy in w_copies:
-        copy.wait()
-    for d in range(1, 8):
-        w_spread.append(
-            remote(wq.at[other, wq_rows, :], wq.at[other, wq_rows, :], piece_device(d))
-        )
-        w_spread[-1].start()
+    w_copies[1].wait()
     for d in range(1, 8):
         w_spread.append(
             remote(wo.at[other, wo_rows, :], wo.at[other, wo_rows, :], piece_device(d))
@@ -421,7 +423,7 @@
         mix[0, rows, :] = mixed[:, 0:HALF]
         mix[1, rows, :] = mixed[:, HALF:CH]
 
-    for copy in w_spread:
+    for copy in w_spread[:7]:
         copy.wait()
 
     @pl.loop(0, EXT // STEP)
@@ -430,6 +432,8 @@
         query[other, rows, :] = dot(normed[rows, :], wq[other]).astype(BF16)
 
     for copy in kv_spread:
+        copy.wait()
+    for copy in w_spread[7:]:
         copy.wait()
 
     @pl.loop(0, EXT // STEP)
@@ -572,26 +576,25 @@
 
     second = [[], []]
 
+    def second_total(c, at):
+        rows = pl.ds(pl.multiple_of(at * 144, 16), 144)
+        return (
+            a1[c, rows, :]
+            + r1[c, 0, rows, :].astype(F32)
+            + r1[c, 1, rows, :].astype(F32)
+            + r1[c, 2, rows, :].astype(F32)
+        )
+
     def second_stage(c):
         for copy in first[c]:
             copy.wait()
-
-        def total(at):
-            rows = pl.ds(pl.multiple_of(at * 144, 16), 144)
-            return (
-                a1[c, rows, :]
-                + r1[c, 0, rows, :].astype(F32)
-                + r1[c, 1, rows, :].astype(F32)
-                + r1[c, 2, rows, :].astype(F32)
-            )
-
         for d in range(1, 4):
-            s2[c, d - 1] = total(lax.rem(v + d, 4)).astype(BF16)
+            s2[c, d - 1] = second_total(c, lax.rem(v + d, 4)).astype(BF16)
             second[c].append(remote(s2.at[c, d - 1], r2.at[c, d - 1], second_device(d)))
             second[c][-1].start()
-        a2[c] = total(v)
 
     second_stage(0)
+    a2[0] = second_total(0, v)
     for copy in second_o:
         copy.wait()
     rows = pl.ds(pl.multiple_of(v * 32, 32), 32)
@@ -605,6 +608,7 @@
         third_o.append(remote(s3o.at[d - 1], r3o.at[d - 1], depth_device(d)))
         third_o[-1].start()
     second_stage(1)
+    a2[1] = second_total(1, v)
     for copy in third_o:
         copy.wait()
     rows = pl.ds(pl.multiple_of(z * 8, 8), 8)
@@ -628,32 +632,36 @@
     for c in range(2):
         for copy in second[c]:
             copy.wait()
-
-    for c in range(2):
         a2[c] = (
             a2[c] + r2[c, 0].astype(F32) + r2[c, 1].astype(F32) + r2[c, 2].astype(F32)
         )
 
-    def third_rows(t):
+    def third_rows(t, k):
         rows = pl.ds(pl.multiple_of(lax.rem(t, 2) * 72, 8), 72)
-        return a2[t // 2, rows, :]
-
-    pad = jnp.zeros((8, STEP), F32)
+        total = a2[t // 2, rows, :]
+        return jnp.where(k == 0, total[0:36], total[36:72])
+
+    pad = jnp.zeros((12, STEP), F32)
     third = []
-    for d in range(1, 4):
-        total = third_rows(lax.rem(z + d, 4))
+    for d in range(8):
+        step, swap = d // 2, d % 2
+        if d == 0:
+            continue
+        k = 1 - core if swap else core
+        total = third_rows(lax.rem(z + step, 4), k)
         s3[d - 1] = jnp.concatenate([total, pad], axis=0).astype(BF16)
-        third.append(remote(s3.at[d - 1], r3.at[d - 1], depth_device(d)))
+        third.append(remote(s3.at[d - 1], r3.at[d - 1], depth_core_device(step, k)))
         third[-1].start()
-    own = third_rows(z)
+    own = third_rows(z, core)
+    first_core = core == 0
     for copy in third:
         copy.wait()
-    arrived = r3[0].astype(F32) + r3[1].astype(F32) + r3[2].astype(F32)
-    own = own + arrived[0:72]
-    a3[...] = own
-    conv_cross = remote(a3, conv_peer, peer_core)
-    conv_cross.start()
-    first_core = core == 0
+    mine = own + r3[1].astype(F32)[0:36] + r3[3].astype(F32)[0:36] + r3[5].astype(F32)[0:36]
+    cross = (
+        r3[0].astype(F32) + r3[2].astype(F32) + r3[4].astype(F32) + r3[6].astype(F32)
+    )[0:36]
+    gconv_out[:, 0:STEP] = jnp.where(first_core, mine, cross)
+    gconv_out[:, STEP:HALF] = jnp.where(first_core, cross, mine)
     for copy in last:
         copy.wait_send()
     for k in range(2):
@@ -668,12 +676,6 @@
         gout_out[:, k * STEP : (k + 1) * STEP] = jnp.where(
             first_core, out_peer[k, 0:4], out_peer[k, 4:8]
         )
-    conv_cross.wait()
-    peer = conv_peer[...]
-    low_half = jnp.where(first_core, own, peer)
-    high_half = jnp.where(first_core, peer, own)
-    gconv_out[:, 0:STEP] = jnp.where(first_core, low_half[0:36], low_half[36:72])
-    gconv_out[:, STEP:HALF] = jnp.where(first_core, high_half[0:36], high_half[36:72])
     put_result.wait()
     assert count[0] == COPIES
 
@@ -689,7 +691,7 @@
         copy.wait()
 
 
-COPIES = 75
+COPIES = 78
 VMEM = pltpu.VMEM
 ANY = pl.BlockSpec(memory_space=pl.ANY)
 INSIDE = pl.BlockSpec(memory_space=pltpu.VMEM)
@@ -776,10 +778,8 @@
             VMEM((2, 3, 144, STEP), BF16),
             VMEM((2, 3, 144, STEP), BF16),
             VMEM((2, 144, STEP), F32),
-            VMEM((3, 80, STEP), BF16),
-            VMEM((3, 80, STEP), BF16),
-            VMEM((72, STEP), F32),
-            VMEM((72, STEP), F32),
+            VMEM((7, 48, STEP), BF16),
+            VMEM((7, 48, STEP), BF16),
             VMEM((2, 512, STEP), F32),
             VMEM((512, STEP), BF16),
             VMEM((512, STEP), BF16),

time: 63.3 us -> 64.2 us (1.014)
  Pallas kernels: 60.5 us -> 61.4 us
    pallas_call x1, Pallas kernels: 58.8 us -> 59.7 us  [shards(): pl.pallas_call(kernel, out_shape=(jax.ShapeDtypeStruct((PIX, HALF), BF16)...]
where the time goes in v3:
time: 64.2 us; the launch traced here: 64 us
  Pallas kernels  61.4 us (96%)
  between operations  1.93 us (3%)
  other arithmetic  0.67 us (1%)
    pallas_call x1, Pallas kernels, shards(): pl.pallas_call(kernel, out_shape=(jax.ShapeDtypeStruct((PIX, HALF), BF16)...  59.7 us
    pallas_call x1, Pallas kernels, shards(): pl.pallas_call(output_kernel, out_shape=(jax.ShapeDtypeStruct((PIX, HALF)...  1.7 us

profile of v3, /device:TPU:1, one launch (start us, length us, event | category | flops | bytes accessed | tf_op | source)
XLA Modules:
  0.0 64.0 jit_solution(16861343654089191883)
XLA Ops:
  1.9 0.7 %fusion.time_in = bf16[1,512]{1,0:T(2,128)(2,1)} fusion(f32[]{:T(128)} %bitcast.4), kind=kLoop, calls=%fused_computation.1 | loop fusion | flops 3584 | bytes 1028 | tf_op jit(solution)/shard_map/convert_element_type | solution.py:706
  2.6 59.7 %block.1 = (bf16[512,256]{1,0:T(8,128)(2,1)}, f32[36,256]{1,0:T(8,128)}, f32[4,256]{1,0:T(4,128)}) custom-call(s32[1]{0:T(128)S(6)} %copy.16.lengths, bf16[512,512]{1,0:T(8,128)(2,1)} %bitcast.7, bf16[128,512]{1,0:T(8,128)(2,1)} %bitcast.9, bf16[32,128]{1,0:T(8,128)(2,1)} %bitcast.10, bf16[4,128]{1,0:T(4,128)(2,1)} %bitcast.11, bf16[1,512]{1,0:T(2,128)(2,1)} %fusion.time_in, ...), custom_call_target="tpu_custom_call" | custom-call | tf_op jit(solution)/shard_map/block/pallas_call | solution.py:725
  62.3 1.7 %outputs.1 = (bf16[512,256]{1,0:T(8,128)(2,1)}, f32[36,256]{1,0:T(8,128)}, f32[4,256]{1,0:T(4,128)}) custom-call(bf16[512,256]{1,0:T(8,128)(2,1)} %get-tuple-element.9.a, f32[36,256]{1,0:T(8,128)} %get-tuple-element.10.b, f32[4,256]{1,0:T(4,128)} %get-tuple-element.11.c), custom_call_target="tpu_custom_call" | custom-call | tf_op jit(solution)/shard_map/outputs/pallas_call | solution.py:819

commit v4 on v3

--- a/solution.py
+++ b/solution.py
@@ -313,13 +313,6 @@
     enc = enc_in[...].astype(F32)
     ld_wk.wait()
     ld_wv.wait()
-    w_spread = []
-    w_copies[0].wait()
-    for d in range(1, 8):
-        w_spread.append(
-            remote(wq.at[other, wq_rows, :], wq.at[other, wq_rows, :], piece_device(d))
-        )
-        w_spread[-1].start()
     for copy in hid_copies:
         copy.wait()
     own_tokens = pl.ds(pl.multiple_of(slab * PIECE, PIECE), PIECE)
@@ -350,7 +343,14 @@
         kv_copies[-1].start()
     gact_inner.start()
 
-    w_copies[1].wait()
+    w_spread = []
+    for copy in w_copies:
+        copy.wait()
+    for d in range(1, 8):
+        w_spread.append(
+            remote(wq.at[other, wq_rows, :], wq.at[other, wq_rows, :], piece_device(d))
+        )
+        w_spread[-1].start()
     for d in range(1, 8):
         w_spread.append(
             remote(wo.at[other, wo_rows, :], wo.at[other, wo_rows, :], piece_device(d))
@@ -492,6 +492,24 @@
         grad_lift = grad_act * gate * (1.0 + lifted * (1.0 - gate))
         gmix[rows, :] = (cot[rows_ext, :].astype(F32) + grad_lift * gain).astype(BF16)
 
+    first = [[], []]
+
+    def first_stage(c):
+        to_core[c].wait()
+        for d in range(1, 4):
+            start = c * 2304 + lax.rem(u + d, 4) * 576
+
+            @pl.loop(0, 4)
+            def _(i):
+                rows = pl.ds(pl.multiple_of(start + i * 144, 16), 144)
+                total = cv[core, rows, :] + core_recv[rows, :].astype(F32)
+                s1[c, d - 1, pl.ds(pl.multiple_of(i * 144, 16), 144), :] = total.astype(BF16)
+
+            first[c].append(remote(s1.at[c, d - 1], r1.at[c, d - 1], first_device(d)))
+            first[c][-1].start()
+
+    first_stage(0)
+
     for to in range(2):
         term = dot_tn(gmix[...], att[to, COLS : COLS + PIX, :])
         for low in range(2):
@@ -506,23 +524,6 @@
     to_core_o = remote(core_send_o, core_recv_o, peer_core)
     to_core_o.start()
 
-    first = [[], []]
-
-    def first_stage(c):
-        to_core[c].wait()
-        for d in range(1, 4):
-            start = c * 2304 + lax.rem(u + d, 4) * 576
-
-            @pl.loop(0, 4)
-            def _(i):
-                rows = pl.ds(pl.multiple_of(start + i * 144, 16), 144)
-                total = cv[core, rows, :] + core_recv[rows, :].astype(F32)
-                s1[c, d - 1, pl.ds(pl.multiple_of(i * 144, 16), 144), :] = total.astype(BF16)
-
-            first[c].append(remote(s1.at[c, d - 1], r1.at[c, d - 1], first_device(d)))
-            first[c][-1].start()
-
-    first_stage(0)
     to_core_o.wait()
     first_o = []
     for d in range(1, 4):

time: 64.2 us -> 62.2 us (0.969)
  Pallas kernels: 61.4 us -> 59.4 us
    pallas_call x1, Pallas kernels: 59.7 us -> 57.7 us  [shards(): pl.pallas_call(kernel, out_shape=(jax.ShapeDtypeStruct((PIX, HALF), BF16)...]
where the time goes in v4:
time: 62.2 us; the launch traced here: 62 us
  Pallas kernels  59.4 us (95%)
  between operations  1.93 us (3%)
  other arithmetic  0.67 us (1%)
    pallas_call x1, Pallas kernels, shards(): pl.pallas_call(kernel, out_shape=(jax.ShapeDtypeStruct((PIX, HALF), BF16)...  57.7 us
    pallas_call x1, Pallas kernels, shards(): pl.pallas_call(output_kernel, out_shape=(jax.ShapeDtypeStruct((PIX, HALF)...  1.7 us

profile of v4, /device:TPU:1, one launch (start us, length us, event | category | flops | bytes accessed | tf_op | source)
XLA Modules:
  0.0 62.0 jit_solution(12482000583660241686)
XLA Ops:
  1.9 0.7 %fusion.time_in = bf16[1,512]{1,0:T(2,128)(2,1)} fusion(f32[]{:T(128)} %bitcast.4), kind=kLoop, calls=%fused_computation.1 | loop fusion | flops 3584 | bytes 1028 | tf_op jit(solution)/shard_map/convert_element_type | solution.py:707
  2.6 57.7 %block.1 = (bf16[512,256]{1,0:T(8,128)(2,1)}, f32[36,256]{1,0:T(8,128)}, f32[4,256]{1,0:T(4,128)}) custom-call(s32[1]{0:T(128)S(6)} %copy.16.lengths, bf16[512,512]{1,0:T(8,128)(2,1)} %bitcast.7, bf16[128,512]{1,0:T(8,128)(2,1)} %bitcast.9, bf16[32,128]{1,0:T(8,128)(2,1)} %bitcast.10, bf16[4,128]{1,0:T(4,128)(2,1)} %bitcast.11, bf16[1,512]{1,0:T(2,128)(2,1)} %fusion.time_in, ...), custom_call_target="tpu_custom_call" | custom-call | tf_op jit(solution)/shard_map/block/pallas_call | solution.py:726
  60.3 1.7 %outputs.1 = (bf16[512,256]{1,0:T(8,128)(2,1)}, f32[36,256]{1,0:T(8,128)}, f32[4,256]{1,0:T(4,128)}) custom-call(bf16[512,256]{1,0:T(8,128)(2,1)} %get-tuple-element.9.a, f32[36,256]{1,0:T(8,128)} %get-tuple-element.10.b, f32[4,256]{1,0:T(4,128)} %get-tuple-element.11.c), custom_call_target="tpu_custom_call" | custom-call | tf_op jit(solution)/shard_map/outputs/pallas_call | solution.py:820

commit v5 on v4

--- a/solution.py
+++ b/solution.py
@@ -25,6 +25,7 @@
 TOK = 128
 PIECE = 16
 STEP = 128
+WIDE = 320
 
 
 def dot(a, b):
@@ -395,7 +396,7 @@
         copy.wait()
     lane = lax.broadcasted_iota(jnp.int32, (TOK, STEP), 1)
     low_lanes = lane < 64
-    live = lax.broadcasted_iota(jnp.int32, (STEP, TOK), 1) < lengths[0]
+    live = lax.broadcasted_iota(jnp.int32, (WIDE, TOK), 1) < lengths[0]
     zero = jnp.zeros((TOK, STEP), BF16)
 
     def attend(group, rows):
@@ -410,14 +411,14 @@
                 scores = jnp.where(live, scores * 0.125, -1e30)
                 peak = jnp.max(scores, axis=-1, keepdims=True)
                 raised = jnp.exp(scores - peak)
-                soft = raised / jnp.sum(raised, axis=-1, keepdims=True)
+                soft = raised * (1.0 / jnp.sum(raised, axis=-1, keepdims=True))
                 term = dot(soft.astype(BF16), jnp.where(keep, values, zero))
                 total = term if total is None else total + term
             att[group, rows, at : at + STEP] = total.astype(BF16)
 
-    @pl.loop(0, EXT // STEP)
+    @pl.loop(0, EXT // WIDE)
     def _(m):
-        rows = pl.ds(pl.multiple_of(m * STEP, STEP), STEP)
+        rows = pl.ds(pl.multiple_of(m * WIDE, COLS), WIDE)
         attend(chan, rows)
         mixed = pix[rows, :].astype(F32) + dot(att[chan, rows, :], wo[chan])
         mix[0, rows, :] = mixed[:, 0:HALF]
@@ -436,9 +437,9 @@
     for copy in w_spread[7:]:
         copy.wait()
 
-    @pl.loop(0, EXT // STEP)
+    @pl.loop(0, EXT // WIDE)
     def _(m):
-        rows = pl.ds(pl.multiple_of(m * STEP, STEP), STEP)
+        rows = pl.ds(pl.multiple_of(m * WIDE, COLS), WIDE)
         attend(other, rows)
         mixed = dot(att[other, rows, :], wo[other])
         mix[0, rows, :] += mixed[:, 0:HALF]

time: 62.2 us -> 57.5 us (0.924)
  Pallas kernels: 59.4 us -> 54.7 us
    pallas_call x1, Pallas kernels: 57.7 us -> 53 us  [shards(): pl.pallas_call(kernel, out_shape=(jax.ShapeDtypeStruct((PIX, HALF), BF16)...]
where the time goes in v5:
time: 57.5 us; the launch traced here: 57.3 us
  Pallas kernels  54.7 us (95%)
  between operations  1.93 us (3%)
  other arithmetic  0.67 us (1%)
    pallas_call x1, Pallas kernels, shards(): pl.pallas_call(kernel, out_shape=(jax.ShapeDtypeStruct((PIX, HALF), BF16)...  53 us
    pallas_call x1, Pallas kernels, shards(): pl.pallas_call(output_kernel, out_shape=(jax.ShapeDtypeStruct((PIX, HALF)...  1.7 us

profile of v5, /device:TPU:1, one launch (start us, length us, event | category | flops | bytes accessed | tf_op | source)
XLA Modules:
  0.0 57.3 jit_solution(10889595955783403909)
XLA Ops:
  1.9 0.7 %fusion.time_in = bf16[1,512]{1,0:T(2,128)(2,1)} fusion(f32[]{:T(128)} %bitcast.4), kind=kLoop, calls=%fused_computation.1 | loop fusion | flops 3584 | bytes 1028 | tf_op jit(solution)/shard_map/convert_element_type | solution.py:708
  2.6 53.0 %block.1 = (bf16[512,256]{1,0:T(8,128)(2,1)}, f32[36,256]{1,0:T(8,128)}, f32[4,256]{1,0:T(4,128)}) custom-call(s32[1]{0:T(128)S(6)} %copy.16.lengths, bf16[512,512]{1,0:T(8,128)(2,1)} %bitcast.7, bf16[128,512]{1,0:T(8,128)(2,1)} %bitcast.9, bf16[32,128]{1,0:T(8,128)(2,1)} %bitcast.10, bf16[4,128]{1,0:T(4,128)(2,1)} %bitcast.11, bf16[1,512]{1,0:T(2,128)(2,1)} %fusion.time_in, ...), custom_call_target="tpu_custom_call" | custom-call | tf_op jit(solution)/shard_map/block/pallas_call | solution.py:727
  55.6 1.7 %outputs.1 = (bf16[512,256]{1,0:T(8,128)(2,1)}, f32[36,256]{1,0:T(8,128)}, f32[4,256]{1,0:T(4,128)}) custom-call(bf16[512,256]{1,0:T(8,128)(2,1)} %get-tuple-element.9.a, f32[36,256]{1,0:T(8,128)} %get-tuple-element.10.b, f32[4,256]{1,0:T(4,128)} %get-tuple-element.11.c), custom_call_target="tpu_custom_call" | custom-call | tf_op jit(solution)/shard_map/outputs/pallas_call | solution.py:821

commit v6 on v5

--- a/solution.py
+++ b/solution.py
@@ -25,7 +25,8 @@
 TOK = 128
 PIECE = 16
 STEP = 128
-WIDE = 320
+WIDE = 640
+GATE = 256
 
 
 def dot(a, b):
@@ -482,10 +483,10 @@
     for copy in gact_edges:
         copy.wait()
 
-    @pl.loop(0, PIX // STEP)
+    @pl.loop(0, PIX // GATE)
     def _(m):
-        rows = pl.ds(pl.multiple_of(m * STEP, STEP), STEP)
-        rows_ext = pl.ds(pl.multiple_of(m * STEP + COLS, COLS), STEP)
+        rows = pl.ds(pl.multiple_of(m * GATE, GATE), GATE)
+        rows_ext = pl.ds(pl.multiple_of(m * GATE + COLS, COLS), GATE)
         gain = 1.0 + film[chan, 0, 0:1, :]
         lifted = mix[chan, rows_ext, :] * gain + film[chan, 1, 0:1, :]
         gate = silu_gate(lifted)

time: 57.5 us -> 57.4 us (level)
  no operation moved by 1% of the time
where the time goes in v6:
time: 57.4 us; the launch traced here: 57.3 us
  Pallas kernels  54.7 us (95%)
  between operations  1.93 us (3%)
  other arithmetic  0.67 us (1%)
    pallas_call x1, Pallas kernels, shards(): pl.pallas_call(kernel, out_shape=(jax.ShapeDtypeStruct((PIX, HALF), BF16)...  53 us
    pallas_call x1, Pallas kernels, shards(): pl.pallas_call(output_kernel, out_shape=(jax.ShapeDtypeStruct((PIX, HALF)...  1.7 us

profile of v6, /device:TPU:1, one launch (start us, length us, event | category | flops | bytes accessed | tf_op | source)
XLA Modules:
  0.0 57.3 jit_solution(1508270878655751437)
XLA Ops:
  1.9 0.7 %fusion.time_in = bf16[1,512]{1,0:T(2,128)(2,1)} fusion(f32[]{:T(128)} %bitcast.4), kind=kLoop, calls=%fused_computation.1 | loop fusion | flops 3584 | bytes 1028 | tf_op jit(solution)/shard_map/convert_element_type | solution.py:709
  2.6 53.0 %block.1 = (bf16[512,256]{1,0:T(8,128)(2,1)}, f32[36,256]{1,0:T(8,128)}, f32[4,256]{1,0:T(4,128)}) custom-call(s32[1]{0:T(128)S(6)} %copy.16.lengths, bf16[512,512]{1,0:T(8,128)(2,1)} %bitcast.7, bf16[128,512]{1,0:T(8,128)(2,1)} %bitcast.9, bf16[32,128]{1,0:T(8,128)(2,1)} %bitcast.10, bf16[4,128]{1,0:T(4,128)(2,1)} %bitcast.11, bf16[1,512]{1,0:T(2,128)(2,1)} %fusion.time_in, ...), custom_call_target="tpu_custom_call" | custom-call | tf_op jit(solution)/shard_map/block/pallas_call | solution.py:728
  55.6 1.7 %outputs.1 = (bf16[512,256]{1,0:T(8,128)(2,1)}, f32[36,256]{1,0:T(8,128)}, f32[4,256]{1,0:T(4,128)}) custom-call(bf16[512,256]{1,0:T(8,128)(2,1)} %get-tuple-element.9.a, f32[36,256]{1,0:T(8,128)} %get-tuple-element.10.b, f32[4,256]{1,0:T(4,128)} %get-tuple-element.11.c), custom_call_target="tpu_custom_call" | custom-call | tf_op jit(solution)/shard_map/outputs/pallas_call | solution.py:822
